TPU v7x, 8 devices: a whole 2x2x1 slice. The times are simulated.
8 devices in a mesh: replica: 2 (over z, y), stage: 4 (over x, core).
Axes of the slice: x: 2, y: 2, z: 1, core: 2. Of those that a mesh axis runs over, the one named last changes fastest.
Arguments:
- embeddings: bfloat16 [3072, 2048], P('replica'), parts along dimension 0
- valid_len: int32 [2], P('replica'), parts along dimension 0
- attn_gain: float32 [4, 2048], P('stage')
- w_q: bfloat16 [4, 2048, 32, 64], P('stage')
- w_k: bfloat16 [4, 2048, 8, 64], P('stage')
- w_v: bfloat16 [4, 2048, 8, 64], P('stage')
- w_o: bfloat16 [4, 32, 64, 2048], P('stage')
- mlp_gain: float32 [4, 2048], P('stage')
- w_gate: bfloat16 [4, 2048, 8192], P('stage')
- w_up: bfloat16 [4, 2048, 8192], P('stage')
- w_down: bfloat16 [4, 8192, 2048], P('stage')
Outputs:
- output 1: bfloat16 [3072, 2048], P(('replica', 'stage')), parts along dimension 0
- output 2: bfloat16 [4, 3072, 8, 64], P('stage', 'replica'), parts along dimension 1
- output 3: bfloat16 [4, 3072, 8, 64], P('stage', 'replica'), parts along dimension 1
There are 2 independent parts. A program takes and returns all parts, laid end to end along the dimension named above; an argument that names none is the same for every part.
All inputs are finite; a program needn't handle non-finite values.
Results may differ from a plain program's by a relative error of at most 0.02.
Values are sent between devices in bfloat16 or wider.
A program may use at most 1 GiB of HBM per device.

v0:
```python
import jax
import jax.numpy as jnp
from jax import lax
from jax.sharding import PartitionSpec as P

EPS = 1e-5
ROPE_BASE = 10000.0
NEG_BIG = -1e30


def rms_norm(hidden, norm_gain):
    hid32 = hidden.astype(jnp.float32)
    inv_rms = lax.rsqrt(jnp.mean(hid32 * hid32, axis=-1, keepdims=True) + EPS)
    return (hid32 * inv_rms * norm_gain).astype(jnp.bfloat16)


def rope_tables(positions, head_dim):
    half_dim = head_dim // 2
    inv_freq = ROPE_BASE ** (-jnp.arange(half_dim, dtype=jnp.float32) * (2.0 / head_dim))
    angles = positions.astype(jnp.float32)[:, None] * inv_freq[None, :]
    return jnp.cos(angles), jnp.sin(angles)


def apply_rope(values, cos_tab, sin_tab):
    half_dim = values.shape[-1] // 2
    front_half = values[..., :half_dim]
    back_half = values[..., half_dim:]
    return jnp.concatenate([front_half * cos_tab - back_half * sin_tab, back_half * cos_tab + front_half * sin_tab], axis=-1)


def project_qkv(normed, layer_idx, params, positions):
    w_q, w_k, w_v = params[1], params[2], params[3]
    d_model, kv_heads, head_dim = w_k.shape[1], w_k.shape[2], w_k.shape[3]
    group_size = w_q.shape[2] // kv_heads
    w_q_heads = w_q[layer_idx].reshape(d_model, kv_heads, group_size, head_dim)
    q_proj = jnp.einsum('sd,dhgk->shgk', normed, w_q_heads, preferred_element_type=jnp.float32)
    k_proj = jnp.einsum('sd,dhk->shk', normed, w_k[layer_idx], preferred_element_type=jnp.float32)
    v_new = jnp.einsum('sd,dhk->shk', normed, w_v[layer_idx], preferred_element_type=jnp.float32).astype(jnp.bfloat16)
    cos_tab, sin_tab = rope_tables(positions, head_dim)
    q_rot = apply_rope(q_proj, cos_tab[:, None, None, :], sin_tab[:, None, None, :]).astype(jnp.bfloat16)
    k_rot = apply_rope(k_proj, cos_tab[:, None, :], sin_tab[:, None, :]).astype(jnp.bfloat16)
    return q_rot, k_rot, v_new


def causal_attention(q_block, key_all, value_all, q_start, n_key_blocks, valid_pos):
    block_len, kv_heads, group_size, head_dim = q_block.shape
    score_scale = head_dim ** -0.5
    q_pos = q_start + jnp.arange(block_len)

    def key_step(block_idx, loop_state):
        run_max, run_sum, acc_out = loop_state
        k_start = block_idx * block_len
        key_blk = lax.dynamic_slice_in_dim(key_all, k_start, block_len, axis=0)
        value_blk = lax.dynamic_slice_in_dim(value_all, k_start, block_len, axis=0)
        scores = jnp.einsum('qhgd,khd->hgqk', q_block, key_blk, preferred_element_type=jnp.float32) * score_scale
        k_pos = k_start + jnp.arange(block_len)
        allowed = (k_pos[None, :] <= q_pos[:, None]) & (k_pos[None, :] < valid_pos)
        scores = jnp.where(allowed, scores, NEG_BIG)
        new_max = jnp.maximum(run_max, jnp.max(scores, axis=-1))
        rescale = jnp.exp(run_max - new_max)
        probs_blk = jnp.exp(scores - new_max[..., None])
        run_sum = run_sum * rescale + jnp.sum(probs_blk, axis=-1)
        acc_out = acc_out * rescale[..., None] + jnp.einsum('hgqk,khd->hgqd', probs_blk.astype(jnp.bfloat16), value_blk, preferred_element_type=jnp.float32)
        return new_max, run_sum, acc_out

    init_state = (jnp.full((kv_heads, group_size, block_len), NEG_BIG, jnp.float32),
                  jnp.zeros((kv_heads, group_size, block_len), jnp.float32),
                  jnp.zeros((kv_heads, group_size, block_len, head_dim), jnp.float32))
    run_max, run_sum, acc_out = lax.fori_loop(0, n_key_blocks, key_step, init_state)
    return (acc_out / run_sum[..., None]).astype(jnp.bfloat16)


def mlp_block(hidden, attn_out, layer_idx, params):
    mlp_gain, w_gate, w_up, w_down = params[5], params[6], params[7], params[8]
    hidden = (hidden.astype(jnp.float32) + attn_out).astype(jnp.bfloat16)
    normed = rms_norm(hidden, mlp_gain[layer_idx])
    gate_proj = jnp.dot(normed, w_gate[layer_idx], preferred_element_type=jnp.float32)
    up_proj = jnp.dot(normed, w_up[layer_idx], preferred_element_type=jnp.float32)
    act_val = (jax.nn.silu(gate_proj) * up_proj).astype(jnp.bfloat16)
    down_proj = jnp.dot(act_val, w_down[layer_idx], preferred_element_type=jnp.float32)
    return (hidden.astype(jnp.float32) + down_proj).astype(jnp.bfloat16)


def block_layer(hidden, layer_idx, params, key_cache, value_cache, blk_index, valid_pos):
    block_len = hidden.shape[0]
    q_start = blk_index * block_len
    normed = rms_norm(hidden, params[0][layer_idx])
    q_rot, k_rot, v_new = project_qkv(normed, layer_idx, params, q_start + jnp.arange(block_len))
    key_cache = lax.dynamic_update_slice(key_cache, k_rot[None], (layer_idx, q_start, 0, 0))
    value_cache = lax.dynamic_update_slice(value_cache, v_new[None], (layer_idx, q_start, 0, 0))
    attn_heads = causal_attention(q_rot, key_cache[layer_idx], value_cache[layer_idx], q_start, blk_index + 1, valid_pos)
    kv_heads, group_size, head_dim = attn_heads.shape[0], attn_heads.shape[1], attn_heads.shape[3]
    w_o_heads = params[4][layer_idx].reshape(kv_heads, group_size, head_dim, -1)
    attn_out = jnp.einsum('hgqd,hgde->qe', attn_heads, w_o_heads, preferred_element_type=jnp.float32)
    return mlp_block(hidden, attn_out, layer_idx, params), key_cache, value_cache


def solution(mesh):
    stages = mesh.shape['stage']
    send_pairs = [(src_stage, src_stage + 1) for src_stage in range(stages - 1)]
    gain_spec = P('stage', None)
    spec_three = P('stage', None, None)
    spec_four = P('stage', None, None, None)

    def stage_program(embeddings, valid_len, attn_gain, w_q, w_k, w_v, w_o, mlp_gain, w_gate, w_up, w_down):
        params = (attn_gain, w_q, w_k, w_v, w_o, mlp_gain, w_gate, w_up, w_down)
        seq_len, d_model = embeddings.shape
        block_len = seq_len // stages
        layers_here = w_q.shape[0]
        cache_shape = (layers_here, seq_len, w_k.shape[2], w_k.shape[3])
        my_stage = lax.axis_index('stage')
        valid_pos = valid_len[0]

        def run_stage(operands):
            hidden, key_cache, value_cache, blk_index = operands
            for layer_idx in range(layers_here):
                hidden, key_cache, value_cache = block_layer(hidden, layer_idx, params, key_cache, value_cache, blk_index, valid_pos)
            return hidden, key_cache, value_cache

        def skip_stage(operands):
            return operands[0], operands[1], operands[2]

        def tick_fn(tick_idx, loop_state):
            recv_buf, key_cache, value_cache, out_blocks = loop_state
            blk_index = tick_idx - my_stage
            active = (blk_index >= 0) & (blk_index < stages)
            blk_index = jnp.clip(blk_index, 0, stages - 1)
            own_block = lax.dynamic_slice_in_dim(embeddings, blk_index * block_len, block_len, axis=0)
            hidden_in = jnp.where(my_stage == 0, own_block, recv_buf)
            hidden_out, key_cache, value_cache = lax.cond(active, run_stage, skip_stage, (hidden_in, key_cache, value_cache, blk_index))
            out_blocks = lax.cond(active & (my_stage == stages - 1),
                                  lambda blocks: lax.dynamic_update_slice(blocks, hidden_out[None], (blk_index, 0, 0)),
                                  lambda blocks: blocks, out_blocks)
            recv_buf = lax.ppermute(hidden_out, 'stage', send_pairs)
            return recv_buf, key_cache, value_cache, out_blocks

        init_state = (jnp.zeros((block_len, d_model), jnp.bfloat16),
                      jnp.zeros(cache_shape, jnp.bfloat16),
                      jnp.zeros(cache_shape, jnp.bfloat16),
                      jnp.zeros((stages, block_len, d_model), jnp.bfloat16))
        recv_buf, key_cache, value_cache, out_blocks = lax.fori_loop(0, 2 * stages - 1, tick_fn, init_state)
        delivered = lax.all_to_all(out_blocks, 'stage', 0, 0, tiled=True)
        return delivered[stages - 1], key_cache, value_cache

    return jax.shard_map(stage_program, mesh=mesh,
                         in_specs=(P('replica', None), P('replica'), gain_spec, spec_four, spec_four, spec_four, spec_four,
                                   gain_spec, spec_three, spec_three, spec_three),
                         out_specs=(P(('replica', 'stage'), None), P('stage', 'replica', None, None), P('stage', 'replica', None, None)),
                         check_vma=False)
```

profile of v0, /device:TPU:7, one launch (start us, length us, event | category | flops | bytes accessed | tf_op | source)
XLA Modules:
  0.0 1591.9 jit_solution(17375994895791888021)
XLA Ops:
  5.6 1513.0 %while.38 = (s32[]{:T(128)}, bf16[384,2048]{1,0:T(8,128)(2,1)S(1)}, bf16[1,1536,8,64]{1,3,2,0:T(8,128)(2,1)S(1)}, bf16[1,1536,8,64]{1,3,2,0:T(8,128)(2,1)}, bf16...) while((s32[]{:T(128)}, bf16[384,2048]{1,0:T(8,128)(2,1)S(1)}, ...), condition=%wide.region_11.12_spmd, body=%wide.region_0.11_spmd.sunk | while | flops 48024002560 | bytes 312036928 | solution.py:141
  44.0 402.6 %collective-permute-done = bf16[384,2048]{1,0:T(8,128)(2,1)S(1)} collective-permute-done((bf16[384,2048]{1,0:T(8,128)(2,1)}, bf16[384,2048]{1,0:T(8,128)(2,1)S(1)}, u32[]{:S(2)}, u32[]{:S(2)}) %collective-permute-start) | collective-permute-done | bytes 1572896 | tf_op jit(solution)/shard_map/while/body/eval_jaxpr/ppermute | solution.py:134
  449.9 133.7 %conditional.4 = ((bf16[384,2048]{1,0:T(8,128)(2,1)}, bf16[1,1536,8,64]{1,3,2,0:T(8,128)(2,1)S(1)}, bf16[1,1536,8,64]{1,3,2,0:T(8,128)(2,1)})) conditional(s32[]{:T(128)} %convert_element_type.131, (bf16[384,2048]{1,0:T(8,128)(2,1)}, bf16[1,1536,8,64]{1,3,2,0:T(8,128)(2,1)S(1)}, bf16[1,1536,8,64]{1,3,2,0:T(8,128)(2,1)}) %tuple.84, ...), branch_computations={%region_1.1_spmd, %region_2.8_spmd} | conditional | flops 48023216128 | bytes 297847808 | solution.py:130
  468.5 33.0 %while.37 = (s32[]{:T(128)}, f32[8,4,384]{2,1,0:T(4,128)S(1)}, f32[8,4,384]{2,1,0:T(4,128)S(1)}, f32[8,4,384,64]{2,3,1,0:T(8,128)}, s32[]{:T(128)}, /*index=5*/s...) while((s32[]{:T(128)}, f32[8,4,384]{2,1,0:T(4,128)S(1)}, ...), condition=%wide.region_7.6_spmd.clone, body=%wide.region_4.5_spmd.clone.sunk | while | flops 1261757952 | bytes 66657228 | solution.py:69
  510.0 22.2 %fusion.23 = f32[384,8192]{1,0:T(8,128)} fusion(bf16[1,2048,8192]{2,1,0:T(8,128)(2,1)} %get-tuple-element.449, bf16[384,2048]{1,0:T(8,128)(2,1)S(1)} %get-tuple-element.582, f32[2048]{0:T(1024)S(1)} %bitcast.131, f32[384]{0:T(512)S(1)} %add_rsqrt_fusion), kind=kOutput, calls=%fused_computation.29 | convolution fusion | flops 12888047616 | bytes 47719936 | tf_op jit(solution)/shard_map/while/body/eval_jaxpr/cond/branch_1_fun/dot_general | solution.py:77
  532.2 29.2 %multiply_convert_fusion.clone.4 = bf16[384,8192]{1,0:T(8,128)(2,1)} fusion(f32[384,8192]{1,0:T(8,128)} %fusion.23, bf16[1,2048,8192]{2,1,0:T(8,128)(2,1)} %get-tuple-element.450, bf16[384,2048]{1,0:T(8,128)(2,1)S(1)} %get-tuple-element.582, f32[2048]{0:T(1024)S(1)} %bitcast.132, f32[384]{0:T(512)S(1)} %add_rsqrt_fusion), kind=kOutput, calls=%fused_computation.31.clone.clone.clone.1 | convolution fusion | flops 12906921984 | bytes 54011392 | tf_op jit(solution)/shard_map/while/body/eval_jaxpr/cond/branch_1_fun/dot_general | solution.py:78
  561.4 22.0 %fusion.36 = bf16[384,2048]{1,0:T(8,128)(2,1)} fusion(bf16[384,2048]{1,0:T(8,128)(2,1)S(1)} %get-tuple-element.582, bf16[1,8192,2048]{2,1,0:T(8,128)(2,1)} %get-tuple-element.451, bf16[384,8192]{1,0:T(8,128)(2,1)} %multiply_convert_fusion.clone.4), kind=kOutput, calls=%fused_computation.47 | convolution fusion | flops 12887261184 | bytes 42991616 | tf_op jit(solution)/shard_map/while/body/eval_jaxpr/cond/branch_1_fun/dot_general | solution.py:80
  587.7 103.6 %collective-permute-done = bf16[384,2048]{1,0:T(8,128)(2,1)S(1)} collective-permute-done((bf16[384,2048]{1,0:T(8,128)(2,1)}, bf16[384,2048]{1,0:T(8,128)(2,1)S(1)}, u32[]{:S(2)}, u32[]{:S(2)}) %collective-permute-start) | collective-permute-done | bytes 1572896 | tf_op jit(solution)/shard_map/while/body/eval_jaxpr/ppermute | solution.py:134
  695.0 167.2 %conditional.4 = ((bf16[384,2048]{1,0:T(8,128)(2,1)}, bf16[1,1536,8,64]{1,3,2,0:T(8,128)(2,1)S(1)}, bf16[1,1536,8,64]{1,3,2,0:T(8,128)(2,1)})) conditional(s32[]{:T(128)} %convert_element_type.131, (bf16[384,2048]{1,0:T(8,128)(2,1)}, bf16[1,1536,8,64]{1,3,2,0:T(8,128)(2,1)S(1)}, bf16[1,1536,8,64]{1,3,2,0:T(8,128)(2,1)}) %tuple.84, ...), branch_computations={%region_1.1_spmd, %region_2.8_spmd} | conditional | flops 48023216128 | bytes 297847808 | solution.py:130
  713.6 66.2 %while.37 = (s32[]{:T(128)}, f32[8,4,384]{2,1,0:T(4,128)S(1)}, f32[8,4,384]{2,1,0:T(4,128)S(1)}, f32[8,4,384,64]{2,3,1,0:T(8,128)}, s32[]{:T(128)}, /*index=5*/s...) while((s32[]{:T(128)}, f32[8,4,384]{2,1,0:T(4,128)S(1)}, ...), condition=%wide.region_7.6_spmd.clone, body=%wide.region_4.5_spmd.clone.sunk | while | flops 1261757952 | bytes 66657228 | solution.py:69
  788.3 22.2 %fusion.23 = f32[384,8192]{1,0:T(8,128)} fusion(bf16[1,2048,8192]{2,1,0:T(8,128)(2,1)} %get-tuple-element.449, bf16[384,2048]{1,0:T(8,128)(2,1)S(1)} %get-tuple-element.582, f32[2048]{0:T(1024)S(1)} %bitcast.131, f32[384]{0:T(512)S(1)} %add_rsqrt_fusion), kind=kOutput, calls=%fused_computation.29 | convolution fusion | flops 12888047616 | bytes 47719936 | tf_op jit(solution)/shard_map/while/body/eval_jaxpr/cond/branch_1_fun/dot_general | solution.py:77
  810.5 29.2 %multiply_convert_fusion.clone.4 = bf16[384,8192]{1,0:T(8,128)(2,1)} fusion(f32[384,8192]{1,0:T(8,128)} %fusion.23, bf16[1,2048,8192]{2,1,0:T(8,128)(2,1)} %get-tuple-element.450, bf16[384,2048]{1,0:T(8,128)(2,1)S(1)} %get-tuple-element.582, f32[2048]{0:T(1024)S(1)} %bitcast.132, f32[384]{0:T(512)S(1)} %add_rsqrt_fusion), kind=kOutput, calls=%fused_computation.31.clone.clone.clone.1 | convolution fusion | flops 12906921984 | bytes 54011392 | tf_op jit(solution)/shard_map/while/body/eval_jaxpr/cond/branch_1_fun/dot_general | solution.py:78
  839.7 22.0 %fusion.36 = bf16[384,2048]{1,0:T(8,128)(2,1)} fusion(bf16[384,2048]{1,0:T(8,128)(2,1)S(1)} %get-tuple-element.582, bf16[1,8192,2048]{2,1,0:T(8,128)(2,1)} %get-tuple-element.451, bf16[384,8192]{1,0:T(8,128)(2,1)} %multiply_convert_fusion.clone.4), kind=kOutput, calls=%fused_computation.47 | convolution fusion | flops 12887261184 | bytes 42991616 | tf_op jit(solution)/shard_map/while/body/eval_jaxpr/cond/branch_1_fun/dot_general | solution.py:80
  866.2 99.6 %collective-permute-done = bf16[384,2048]{1,0:T(8,128)(2,1)S(1)} collective-permute-done((bf16[384,2048]{1,0:T(8,128)(2,1)}, bf16[384,2048]{1,0:T(8,128)(2,1)S(1)}, u32[]{:S(2)}, u32[]{:S(2)}) %collective-permute-start) | collective-permute-done | bytes 1572896 | tf_op jit(solution)/shard_map/while/body/eval_jaxpr/ppermute | solution.py:134
  969.1 200.0 %conditional.4 = ((bf16[384,2048]{1,0:T(8,128)(2,1)}, bf16[1,1536,8,64]{1,3,2,0:T(8,128)(2,1)S(1)}, bf16[1,1536,8,64]{1,3,2,0:T(8,128)(2,1)})) conditional(s32[]{:T(128)} %convert_element_type.131, (bf16[384,2048]{1,0:T(8,128)(2,1)}, bf16[1,1536,8,64]{1,3,2,0:T(8,128)(2,1)S(1)}, bf16[1,1536,8,64]{1,3,2,0:T(8,128)(2,1)}) %tuple.84, ...), branch_computations={%region_1.1_spmd, %region_2.8_spmd} | conditional | flops 48023216128 | bytes 297847808 | solution.py:130
  987.8 99.2 %while.37 = (s32[]{:T(128)}, f32[8,4,384]{2,1,0:T(4,128)S(1)}, f32[8,4,384]{2,1,0:T(4,128)S(1)}, f32[8,4,384,64]{2,3,1,0:T(8,128)}, s32[]{:T(128)}, /*index=5*/s...) while((s32[]{:T(128)}, f32[8,4,384]{2,1,0:T(4,128)S(1)}, ...), condition=%wide.region_7.6_spmd.clone, body=%wide.region_4.5_spmd.clone.sunk | while | flops 1261757952 | bytes 66657228 | solution.py:69
  1095.5 22.4 %fusion.23 = f32[384,8192]{1,0:T(8,128)} fusion(bf16[1,2048,8192]{2,1,0:T(8,128)(2,1)} %get-tuple-element.449, bf16[384,2048]{1,0:T(8,128)(2,1)S(1)} %get-tuple-element.582, f32[2048]{0:T(1024)S(1)} %bitcast.131, f32[384]{0:T(512)S(1)} %add_rsqrt_fusion), kind=kOutput, calls=%fused_computation.29 | convolution fusion | flops 12888047616 | bytes 47719936 | tf_op jit(solution)/shard_map/while/body/eval_jaxpr/cond/branch_1_fun/dot_general | solution.py:77
  1117.9 29.2 %multiply_convert_fusion.clone.4 = bf16[384,8192]{1,0:T(8,128)(2,1)} fusion(f32[384,8192]{1,0:T(8,128)} %fusion.23, bf16[1,2048,8192]{2,1,0:T(8,128)(2,1)} %get-tuple-element.450, bf16[384,2048]{1,0:T(8,128)(2,1)S(1)} %get-tuple-element.582, f32[2048]{0:T(1024)S(1)} %bitcast.132, f32[384]{0:T(512)S(1)} %add_rsqrt_fusion), kind=kOutput, calls=%fused_computation.31.clone.clone.clone.1 | convolution fusion | flops 12906921984 | bytes 54011392 | tf_op jit(solution)/shard_map/while/body/eval_jaxpr/cond/branch_1_fun/dot_general | solution.py:78
  1173.3 101.5 %collective-permute-done = bf16[384,2048]{1,0:T(8,128)(2,1)S(1)} collective-permute-done((bf16[384,2048]{1,0:T(8,128)(2,1)}, bf16[384,2048]{1,0:T(8,128)(2,1)S(1)}, u32[]{:S(2)}, u32[]{:S(2)}) %collective-permute-start) | collective-permute-done | bytes 1572896 | tf_op jit(solution)/shard_map/while/body/eval_jaxpr/ppermute | solution.py:134
  1278.2 233.2 %conditional.4 = ((bf16[384,2048]{1,0:T(8,128)(2,1)}, bf16[1,1536,8,64]{1,3,2,0:T(8,128)(2,1)S(1)}, bf16[1,1536,8,64]{1,3,2,0:T(8,128)(2,1)})) conditional(s32[]{:T(128)} %convert_element_type.131, (bf16[384,2048]{1,0:T(8,128)(2,1)}, bf16[1,1536,8,64]{1,3,2,0:T(8,128)(2,1)S(1)}, bf16[1,1536,8,64]{1,3,2,0:T(8,128)(2,1)}) %tuple.84, ...), branch_computations={%region_1.1_spmd, %region_2.8_spmd} | conditional | flops 48023216128 | bytes 297847808 | solution.py:130
  1296.9 132.4 %while.37 = (s32[]{:T(128)}, f32[8,4,384]{2,1,0:T(4,128)S(1)}, f32[8,4,384]{2,1,0:T(4,128)S(1)}, f32[8,4,384,64]{2,3,1,0:T(8,128)}, s32[]{:T(128)}, /*index=5*/s...) while((s32[]{:T(128)}, f32[8,4,384]{2,1,0:T(4,128)S(1)}, ...), condition=%wide.region_7.6_spmd.clone, body=%wide.region_4.5_spmd.clone.sunk | while | flops 1261757952 | bytes 66657228 | solution.py:69
  1437.8 22.2 %fusion.23 = f32[384,8192]{1,0:T(8,128)} fusion(bf16[1,2048,8192]{2,1,0:T(8,128)(2,1)} %get-tuple-element.449, bf16[384,2048]{1,0:T(8,128)(2,1)S(1)} %get-tuple-element.582, f32[2048]{0:T(1024)S(1)} %bitcast.131, f32[384]{0:T(512)S(1)} %add_rsqrt_fusion), kind=kOutput, calls=%fused_computation.29 | convolution fusion | flops 12888047616 | bytes 47719936 | tf_op jit(solution)/shard_map/while/body/eval_jaxpr/cond/branch_1_fun/dot_general | solution.py:77
  1460.0 29.2 %multiply_convert_fusion.clone.4 = bf16[384,8192]{1,0:T(8,128)(2,1)} fusion(f32[384,8192]{1,0:T(8,128)} %fusion.23, bf16[1,2048,8192]{2,1,0:T(8,128)(2,1)} %get-tuple-element.450, bf16[384,2048]{1,0:T(8,128)(2,1)S(1)} %get-tuple-element.582, f32[2048]{0:T(1024)S(1)} %bitcast.132, f32[384]{0:T(512)S(1)} %add_rsqrt_fusion), kind=kOutput, calls=%fused_computation.31.clone.clone.clone.1 | convolution fusion | flops 12906921984 | bytes 54011392 | tf_op jit(solution)/shard_map/while/body/eval_jaxpr/cond/branch_1_fun/dot_general | solution.py:78
  1518.7 71.6 %all_to_all.5 = bf16[4,384,2048]{2,1,0:T(8,128)(2,1)S(1)} all-to-all(bf16[4,384,2048]{2,1,0:T(8,128)(2,1)} %get-tuple-element.918), channel_id=1, replica_groups=mesh['replica'=2,'stage'=4] {'stage'}, dimensions={0} | all-to-all | bytes 12582912 | tf_op jit(solution)/shard_map/all_to_all | solution.py:142
  (244 shorter events, 567.5 us)
Async XLA Ops:
  15.1 5.3 copy-start.3
  15.1 5.3 collective-permute-start
  23.6 15.9 copy-start.3
  23.6 15.9 collective-permute-start
  42.6 404.1 %copy-start.3 = (f32[1,2048]{1,0:T(1,128)S(1)}, f32[1,2048]{1,0:T(1,128)}, u32[]{:S(2)}) copy-start(f32[1,2048]{1,0:T(1,128)} %get-tuple-element.939) | copy-start | bytes 24580 | tf_op jit(solution)/shard_map/while
  42.6 404.1 %collective-permute-start = (bf16[384,2048]{1,0:T(8,128)(2,1)}, bf16[384,2048]{1,0:T(8,128)(2,1)S(1)}, u32[]{:S(2)}, u32[]{:S(2)}) collective-permute-start(bf16[384,2048]{1,0:T(8,128)(2,1)} %get-tuple-element.765), channel_id=1, source_target_pairs={{0,1},{1,2},{2,3},{4,5},{5,6},{6,7}} | collective-permute-start | bytes 4718600 | tf_op jit(solution)/shard_map/while/body/eval_jaxpr/ppermute | solution.py:134
  452.0 7.5 slice-start
  455.5 3.9 slice-start.1
  583.6 107.7 %copy-start.3 = (f32[1,2048]{1,0:T(1,128)S(1)}, f32[1,2048]{1,0:T(1,128)}, u32[]{:S(2)}) copy-start(f32[1,2048]{1,0:T(1,128)} %get-tuple-element.939) | copy-start | bytes 24580 | tf_op jit(solution)/shard_map/while
  583.6 107.7 %collective-permute-start = (bf16[384,2048]{1,0:T(8,128)(2,1)}, bf16[384,2048]{1,0:T(8,128)(2,1)S(1)}, u32[]{:S(2)}, u32[]{:S(2)}) collective-permute-start(bf16[384,2048]{1,0:T(8,128)(2,1)} %get-tuple-element.765), channel_id=1, source_target_pairs={{0,1},{1,2},{2,3},{4,5},{5,6},{6,7}} | collective-permute-start | bytes 4718600 | tf_op jit(solution)/shard_map/while/body/eval_jaxpr/ppermute | solution.py:134
  697.1 3.6 copy-start.1
  697.1 7.5 slice-start
  700.7 3.9 slice-start.1
  862.2 103.6 %copy-start.3 = (f32[1,2048]{1,0:T(1,128)S(1)}, f32[1,2048]{1,0:T(1,128)}, u32[]{:S(2)}) copy-start(f32[1,2048]{1,0:T(1,128)} %get-tuple-element.939) | copy-start | bytes 24580 | tf_op jit(solution)/shard_map/while
  862.2 103.6 %collective-permute-start = (bf16[384,2048]{1,0:T(8,128)(2,1)}, bf16[384,2048]{1,0:T(8,128)(2,1)S(1)}, u32[]{:S(2)}, u32[]{:S(2)}) collective-permute-start(bf16[384,2048]{1,0:T(8,128)(2,1)} %get-tuple-element.765), channel_id=1, source_target_pairs={{0,1},{1,2},{2,3},{4,5},{5,6},{6,7}} | collective-permute-start | bytes 4718600 | tf_op jit(solution)/shard_map/while/body/eval_jaxpr/ppermute | solution.py:134
  971.2 7.5 slice-start
  974.8 3.9 slice-start.1
  1169.2 105.6 %copy-start.3 = (f32[1,2048]{1,0:T(1,128)S(1)}, f32[1,2048]{1,0:T(1,128)}, u32[]{:S(2)}) copy-start(f32[1,2048]{1,0:T(1,128)} %get-tuple-element.939) | copy-start | bytes 24580 | tf_op jit(solution)/shard_map/while
  1169.2 105.6 %collective-permute-start = (bf16[384,2048]{1,0:T(8,128)(2,1)}, bf16[384,2048]{1,0:T(8,128)(2,1)S(1)}, u32[]{:S(2)}, u32[]{:S(2)}) collective-permute-start(bf16[384,2048]{1,0:T(8,128)(2,1)} %get-tuple-element.765), channel_id=1, source_target_pairs={{0,1},{1,2},{2,3},{4,5},{5,6},{6,7}} | collective-permute-start | bytes 4718600 | tf_op jit(solution)/shard_map/while/body/eval_jaxpr/ppermute | solution.py:134
  1280.3 7.5 slice-start
  1283.9 3.9 slice-start.1
  1511.4 5.3 copy-start.3
  1511.4 5.3 collective-permute-start
  1518.6 71.6 %copy-start = (bf16[1,1536,8,64]{1,3,2,0:T(8,128)(2,1)}, bf16[1,1536,8,64]{1,3,2,0:T(8,128)(2,1)S(1)}, u32[]{:S(2)}) copy-start(bf16[1,1536,8,64]{1,3,2,0:T(8,128)(2,1)S(1)} %get-tuple-element.916) | copy-start | bytes 4718596
  (5 other events, 17.6 us)
where the time goes:
time: 1600 us; the launch traced here: 1590 us
  waiting for transfers between devices  727 us (45%)
  matrix products  596 us (37%)
  other arithmetic  149 us (9%)
  blocking collectives  71.6 us (4%)
  local copies, waits for them, and re-layouts  25.9 us (2%)
    ppermute x7, waiting for transfers between devices, tick_fn(): recv_buf = lax.ppermute(hidden_out, 'stage', send_pairs)  727 us
    dot_general x10, matrix products, key_step(): jnp.einsum('hgqk,khd->hgqd', probs_blk.astype(jnp.bfloat16), value_blk, p...  138 us
    dot_general x4, matrix products, mlp_block(): jnp.dot(normed, w_up[layer_idx], preferred_element_type=jnp.float32)  117 us
    reduce_sum x10, other arithmetic, key_step(): run_sum = run_sum * rescale + jnp.sum(probs_blk, axis=-1)  103 us
    dot_general x4, matrix products, mlp_block(): jnp.dot(normed, w_gate[layer_idx], preferred_element_type=jnp.float32)  89 us
    dot_general x4, matrix products, mlp_block(): jnp.dot(act_val, w_down[layer_idx], preferred_element_type=jnp.float32)  87.8 us
    dot_general x10, matrix products, key_step(): jnp.einsum('qhgd,khd->hgqk', q_block, key_blk, preferred_element_type=jnp...  80.1 us
    all_to_all x1, blocking collectives, stage_program(): delivered = lax.all_to_all(out_blocks, 'stage', 0, 0, tiled=True)  71.6 us
  transfers between devices with their start and end apart: 7, of which 7 were waited for; matrix products, arithmetic and copies ran while one was open for 1% of the time, Pallas kernels for 0%

commit v1 on v0

v1 whole, which is shorter than its diff:
```python
import math

import jax
import jax.numpy as jnp
import numpy as np
from jax import lax
from jax.experimental import pallas as pl
from jax.experimental.pallas import tpu as pltpu
from jax.sharding import PartitionSpec as P

EPS = 1e-5
ROPE_BASE = 10000.0
NEG = -1e30

SEQ = 1536
D = 2048
HEADS = 32
KV = 8
HD = 64
FF = 8192
STAGES = 4
B = 192
NB = SEQ // B
F = 512
NC = FF // F
NG = NB * NC
VMIN = 768
VMAX = 1344
KEYMAX = VMAX // B
RG = 4
RD = 3
EXP_SCALE = math.log2(math.e)

F32 = jnp.float32
BF16 = jnp.bfloat16


def rope_tables():
    inv_freq = ROPE_BASE ** (-np.arange(HD // 2, dtype=np.float64) * (2.0 / HD))
    angles = inv_freq[:, None] * np.arange(SEQ, dtype=np.float64)[None, :]
    tab = np.zeros((NB, 2, HD // 2, 256), np.float32)
    for blk in range(NB):
        cols = slice(blk * B, (blk + 1) * B)
        tab[blk, 0, :, :B] = np.cos(angles[:, cols])
        tab[blk, 1, :, :B] = np.sin(angles[:, cols])
    return tab


def dot(a, b):
    return jnp.dot(a, b, preferred_element_type=F32)


def stage_kernel(emb, valid, again, wq, wk, wv, wo, mgain, wg, wu, wd, tab_hbm,
                 hid, kout, vout,
                 tab, wqkv_v, wo_v, wg_r, wu_r, wd_r, resid, kc, kT, vT, act, aT, qT, y, sbuf, ffa,
                 mask_x, mask_y, vbias,
                 w_sem, tab_sem, g_sem, u_sem, d_sem, in_sem, send_sem, kv_sem, out_sem):
    stage = lax.axis_index("stage")
    barrier = pltpu.get_barrier_semaphore()
    for k in range(1, STAGES):
        pl.semaphore_signal(barrier, inc=1, device_id={"stage": lax.rem(stage + k, STAGES)},
                            device_id_type=pl.DeviceIdType.MESH)

    def emb_copy(i):
        return pltpu.make_async_copy(emb.at[pl.ds(pl.multiple_of(i * B, B), B), :], resid.at[i], in_sem.at[i])

    def w_copy(p):
        if p < 4:
            src = wq.at[pl.ds(p * 512, 512), :]
        elif p == 4:
            src = wk
        elif p == 5:
            src = wv
        else:
            src = wo.at[pl.ds((p - 6) * 512, 512), :]
        dst = wqkv_v.at[pl.ds(p * 512, 512), :] if p < 6 else wo_v.at[pl.ds((p - 6) * 512, 512), :]
        return pltpu.make_async_copy(src, dst, w_sem.at[p])

    def g_copy(g):
        cols = pl.ds(pl.multiple_of(lax.rem(g, NC) * F, F), F)
        slot = lax.rem(g, RG)
        return pltpu.make_async_copy(wg.at[:, cols], wg_r.at[slot], g_sem.at[slot])

    def u_copy(g):
        cols = pl.ds(pl.multiple_of(lax.rem(g, NC) * F, F), F)
        slot = lax.rem(g, RG)
        return pltpu.make_async_copy(wu.at[:, cols], wu_r.at[slot], u_sem.at[slot])

    def d_copy(g):
        rows = pl.ds(pl.multiple_of(lax.rem(g, NC) * F, F), F)
        slot = lax.rem(g, RD)
        return pltpu.make_async_copy(wd.at[rows, :], wd_r.at[slot], d_sem.at[slot])

    tab_copy = pltpu.make_async_copy(tab_hbm, tab, tab_sem)

    @pl.when(stage == 0)
    def _():
        emb_copy(0).start()

    w_copy(0).start()
    tab_copy.start()
    for p in range(1, 10):
        w_copy(p).start()
    for g in range(RG - 1):
        g_copy(g).start()
        u_copy(g).start()
    d_copy(0).start()

    act[pl.ds(B, 256 - B), :] = jnp.zeros((256 - B, D), BF16)
    for g in range(KV):
        qT[g, pl.ds((1 - g % 2) * HD, HD), :] = jnp.zeros((HD, 4 * B), BF16)
    valid_pos = valid[0]
    vrow = lax.broadcasted_iota(jnp.int32, vbias.shape, 0) + VMIN
    vbias[...] = jnp.where(vrow < valid_pos, 0.0, NEG).astype(F32)
    tab_copy.wait()
    pl.semaphore_wait(barrier, STAGES - 1)

    def norm(i, gain_ref):
        for r in range(0, B, 16):
            x = resid[i, pl.ds(r, 16), :].astype(F32)
            inv = lax.rsqrt(jnp.mean(x * x, axis=-1, keepdims=True) + EPS)
            act[pl.ds(r, 16), :] = (x * inv * gain_ref[...]).astype(BF16)

    def rope(x, cos, sin):
        front = x[:HD // 2]
        back = x[HD // 2:]
        return front * cos - back * sin, back * cos + front * sin

    def put_tokens(ref, i, rows, val):
        base = (i // 2) * (2 * B)
        lo = pl.multiple_of(base, 128)

        @pl.when(lax.rem(i, 2) == 0)
        def _():
            ref[rows, pl.ds(lo, 256)] = val.astype(BF16)

        @pl.when(lax.rem(i, 2) == 1)
        def _():
            rolled = pltpu.roll(val, 64, 1)
            lane = lax.broadcasted_iota(jnp.int32, (val.shape[0], 128), 1)
            mid = pl.multiple_of(base + 128, 128)
            old = ref[rows, pl.ds(mid, 128)].astype(F32)
            ref[rows, pl.ds(mid, 128)] = jnp.where(lane < 64, old, rolled[:, :128]).astype(BF16)
            hi = pl.multiple_of(base + 256, 128)
            ref[rows, pl.ds(hi, 128)] = rolled[:, 128:].astype(BF16)

    def project(i):
        for n in range(8):
            aT[pl.ds(n * 256, 256), :] = act[:, pl.ds(n * 256, 256)].T
        cos = tab[i, 0]
        sin = tab[i, 1]
        lane = lax.broadcasted_iota(jnp.int32, (HD, 128), 1)

        def q_pair(pair, _):
            rows = pl.ds(pl.multiple_of(pair * 512, 512), 512)
            qt = dot(wqkv_v[rows, :], aT[...])
            for gg in range(2):
                heads = []
                for h in range(4):
                    f, b = rope(qt[(gg * 4 + h) * HD:(gg * 4 + h + 1) * HD], cos, sin)
                    heads.append(jnp.concatenate([f, b], axis=0) * 0.125)
                lead = [x[:, :128] for x in heads]
                tail = [x[:, 128:] for x in heads]
                lead.append(jnp.where(lane < 64, tail[0], pltpu.roll(tail[1], 64, 1)))
                lead.append(jnp.where(lane < 64, tail[2], pltpu.roll(tail[3], 64, 1)))
                for t in range(6):
                    qT[pair * 2 + gg, pl.ds(gg * HD, HD), pl.ds(t * 128, 128)] = lead[t].astype(BF16)
            return 0

        lax.fori_loop(0, 4, q_pair, 0)

        for half in range(2):
            kt = dot(wqkv_v[pl.ds(2048 + half * 256, 256), :], aT[...])
            parts = []
            for h in range(4):
                parts += list(rope(kt[h * HD:(h + 1) * HD], cos, sin))
            kt = jnp.concatenate(parts, axis=0)
            put_tokens(kT, i, pl.ds(half * 256, 256), kt)
            kc[pl.ds(pl.multiple_of(i * B, B), B), pl.ds(half * 256, 256)] = kt.astype(BF16).T[:B]
        for half in range(2):
            vt = dot(wqkv_v[pl.ds(2560 + half * 256, 256), :], aT[...])
            put_tokens(vT, i, pl.ds(half * 256, 256), vt)

    def masks(i):
        key = lax.broadcasted_iota(jnp.int32, (128, 128), 0)
        tok = lax.broadcasted_iota(jnp.int32, (128, 128), 1)
        ok = (key <= tok) & (key + i * B < valid_pos)
        mask_x[...] = jnp.where(ok, 0.0, NEG).astype(F32)
        key = lax.broadcasted_iota(jnp.int32, (B, 128), 0)
        tok = lax.broadcasted_iota(jnp.int32, (B, 128), 1)
        tok = 128 + jnp.where(tok < 64, tok, tok - 64)
        ok = (key <= tok) & (key + i * B < valid_pos)
        mask_y[...] = jnp.where(ok, 0.0, NEG).astype(F32)

    def attend(n):
        chunks = min(n + 1, KEYMAX)

        def group(g, _):
            kcols = pl.ds(pl.multiple_of((g // 2) * 128, 128), 128)
            outs = []
            for t in range(3):
                sref = y if t == 0 else sbuf.at[t - 1]
                q = qT[g, :, pl.ds(t * 256, 256)]
                m = None
                spans = []
                for c in range(chunks):
                    rows = 128 if (c == n and t < 2) else B
                    s = dot(kc[pl.ds(c * B, rows), kcols], q)
                    if c == n:
                        mk = mask_x[...] if t < 2 else mask_y[...]
                        s = s + jnp.concatenate([mk, mk], axis=1)
                    elif c * B >= VMIN:
                        mk = vbias[pl.ds(c * B - VMIN, B), :]
                        s = s + jnp.concatenate([mk, mk], axis=1)
                    sref[pl.ds(c * B, rows), :] = s
                    cm = jnp.max(s.reshape(rows // 8, 8, 256), axis=0)
                    m = cm if m is None else jnp.maximum(m, cm)
                    spans.append((c * B, rows))
                mc = jnp.max(m, axis=0, keepdims=True) * EXP_SCALE
                l = None
                probs = []
                for start, rows in spans:
                    p = jnp.exp2(sref[pl.ds(start, rows), :] * EXP_SCALE - mc)
                    ls = jnp.sum(p.reshape(rows // 8, 8, 256), axis=0)
                    l = ls if l is None else l + ls
                    probs.append(p.astype(BF16))
                total = spans[-1][0] + spans[-1][1]
                o = dot(vT[pl.ds(pl.multiple_of(g * HD, HD), HD), pl.ds(0, total)], jnp.concatenate(probs, axis=0))
                outs.append(o * (1.0 / jnp.sum(l, axis=0, keepdims=True)))
            lead = jnp.concatenate([outs[0][:, :128], outs[0][:, 128:], outs[1][:, :128], outs[1][:, 128:]], axis=0)
            t0 = outs[2][:, :128]
            t1 = outs[2][:, 128:]
            tail = jnp.concatenate([t0, pltpu.roll(t0, 64, 1), t1, pltpu.roll(t1, 64, 1)], axis=0)
            ocols = pl.ds(pl.multiple_of(g * 256, 256), 256)
            act[pl.ds(0, 128), ocols] = lead.astype(BF16).T
            act[pl.ds(128, 64), ocols] = tail.astype(BF16).T[:64]
            return 0

        lax.fori_loop(0, KV, group, 0)

    def out_proj(i):
        for n in range(4):
            cols = pl.ds(n * 512, 512)
            o = dot(act[pl.ds(0, B), :], wo_v[:, cols])
            resid[i, :, cols] = (resid[i, :, cols].astype(F32) + o).astype(BF16)

    def gate_up(g):
        g_copy(g).wait()
        u_copy(g).wait()

        @pl.when(g + RG - 1 < NG)
        def _():
            g_copy(g + RG - 1).start()
            u_copy(g + RG - 1).start()

        @pl.when(g + 1 < NG)
        def _():
            d_copy(g + 1).start()

        slot = lax.rem(g, RG)
        x = act[pl.ds(0, B), :]
        gate = dot(x, wg_r[slot])
        up = dot(x, wu_r[slot])
        ffa[lax.rem(g, 2)] = (gate * jax.nn.sigmoid(gate) * up).astype(BF16)

    def down(g):
        slot = lax.rem(g, RD)
        x = ffa[lax.rem(g, 2)]
        for n in range(8):
            rows = pl.ds(n * B, B)
            y[rows, :] = y[rows, :] + dot(x, wd_r[slot, :, pl.ds(n * 256, 256)])

    def mlp(i):
        for n in range(8):
            y[pl.ds(n * B, B), :] = resid[i, :, pl.ds(n * 256, 256)].astype(F32)
        g0 = i * NC
        gate_up(g0)

        def step(c, _):
            g = g0 + c
            d_copy(g - 1).wait()
            gate_up(g)
            down(g - 1)
            return 0

        lax.fori_loop(1, NC, step, 0)
        d_copy(g0 + NC - 1).wait()
        down(g0 + NC - 1)
        for n in range(8):
            resid[i, :, pl.ds(n * 256, 256)] = y[pl.ds(n * B, B), :].astype(BF16)

    def next_copy(i):
        return pltpu.make_async_remote_copy(resid.at[i], resid.at[i], send_sem.at[i], in_sem.at[i],
                                            device_id={"stage": lax.rem(stage + 1, STAGES)},
                                            device_id_type=pl.DeviceIdType.MESH)

    def owner_copy(i):
        part = lax.rem(i, 2)
        return pltpu.make_async_remote_copy(resid.at[i], hid.at[pl.ds(pl.multiple_of(part * B, B), B), :],
                                            send_sem.at[i], out_sem.at[part],
                                            device_id={"stage": i // 2}, device_id_type=pl.DeviceIdType.MESH)

    def own_copy(i):
        part = lax.rem(i, 2)
        return pltpu.make_async_copy(resid.at[i], hid.at[pl.ds(pl.multiple_of(part * B, B), B), :], out_sem.at[part])

    def kv_copy(j, which):
        cols = pl.ds(pl.multiple_of(j * 2 * B, 2 * B), 2 * B)
        src, dst = ((kT, kout), (vT, vout))[which]
        return pltpu.make_async_copy(src.at[:, cols], dst.at[:, cols], kv_sem.at[which, j])

    def block(i, _):
        emb_copy(i).wait()

        @pl.when((stage == 0) & (i + 1 < NB))
        def _():
            emb_copy(i + 1).start()

        norm(i, again)

        @pl.when(i == 0)
        def _():
            for p in range(6):
                w_copy(p).wait()

        project(i)
        masks(i)
        for n in range(NB):
            @pl.when(i == n)
            def _():
                attend(n)

        @pl.when(i == 0)
        def _():
            for p in range(6, 10):
                w_copy(p).wait()

        out_proj(i)
        norm(i, mgain)
        mlp(i)

        @pl.when(lax.rem(i, 2) == 1)
        def _():
            kv_copy(i // 2, 0).start()
            kv_copy(i // 2, 1).start()

        @pl.when(stage < STAGES - 1)
        def _():
            next_copy(i).start()

        @pl.when((stage == STAGES - 1) & (i < NB - 2))
        def _():
            owner_copy(i).start()

        @pl.when((stage == STAGES - 1) & (i >= NB - 2))
        def _():
            own_copy(i).start()

        return 0

    lax.fori_loop(0, NB, block, 0)

    @pl.when(stage < STAGES - 1)
    def _():
        for i in range(NB):
            next_copy(i).wait_send()

    @pl.when(stage == STAGES - 1)
    def _():
        for i in range(NB - 2):
            owner_copy(i).wait_send()

    for part in range(2):
        own_copy(part).wait()
    for j in range(NB // 2):
        kv_copy(j, 0).wait()
        kv_copy(j, 1).wait()


def solution(mesh):
    gain_spec = P('stage', None)
    spec_three = P('stage', None, None)
    spec_four = P('stage', None, None, None)
    table = rope_tables()
    dma = pltpu.SemaphoreType.DMA

    def stage_program(embeddings, valid_len, attn_gain, w_q, w_k, w_v, w_o, mlp_gain, w_gate, w_up, w_down):
        wq = w_q[0].transpose(1, 2, 0).reshape(HEADS * HD, D)
        wk = w_k[0].transpose(1, 2, 0).reshape(KV * HD, D)
        wv = w_v[0].transpose(1, 2, 0).reshape(KV * HD, D)
        wo = w_o[0].reshape(HEADS * HD, D)
        any_spec = pl.BlockSpec(memory_space=pl.ANY)
        vmem_spec = pl.BlockSpec(memory_space=pltpu.VMEM)
        smem_spec = pl.BlockSpec(memory_space=pltpu.SMEM)
        hid, k_t, v_t = pl.pallas_call(
            stage_kernel,
            name="stage_pipeline",
            out_shape=(jax.ShapeDtypeStruct((SEQ // STAGES, D), BF16),
                       jax.ShapeDtypeStruct((KV * HD, SEQ), BF16),
                       jax.ShapeDtypeStruct((KV * HD, SEQ), BF16)),
            in_specs=[any_spec, smem_spec, vmem_spec, any_spec, any_spec, any_spec, any_spec, vmem_spec,
                      any_spec, any_spec, any_spec, any_spec],
            out_specs=(any_spec, any_spec, any_spec),
            scratch_shapes=[
                pltpu.VMEM((NB, 2, HD // 2, 256), F32),
                pltpu.VMEM((3072, D), BF16),
                pltpu.VMEM((D, D), BF16),
                pltpu.VMEM((RG, D, F), BF16),
                pltpu.VMEM((RG, D, F), BF16),
                pltpu.VMEM((RD, F, D), BF16),
                pltpu.VMEM((NB, B, D), BF16),
                pltpu.VMEM((SEQ, KV * HD), BF16),
                pltpu.VMEM((KV * HD, SEQ), BF16),
                pltpu.VMEM((KV * HD, SEQ), BF16),
                pltpu.VMEM((256, D), BF16),
                pltpu.VMEM((D, 256), BF16),
                pltpu.VMEM((KV, 2 * HD, 4 * B), BF16),
                pltpu.VMEM((8 * B, 256), F32),
                pltpu.VMEM((2, VMAX, 256), F32),
                pltpu.VMEM((2, B, F), BF16),
                pltpu.VMEM((128, 128), F32),
                pltpu.VMEM((B, 128), F32),
                pltpu.VMEM((VMAX - VMIN, 128), F32),
                dma((10,)), dma, dma((RG,)), dma((RG,)), dma((RD,)), dma((NB,)), dma((NB,)),
                dma((2, NB // 2)), dma((2,)),
            ],
            compiler_params=pltpu.CompilerParams(collective_id=0, has_side_effects=True,
                                                 vmem_limit_bytes=67043328),
        )(embeddings, valid_len, attn_gain, wq, wk, wv, wo, mlp_gain, w_gate[0], w_up[0], w_down[0],
          jnp.asarray(table))

        def to_cache(x):
            return x.reshape(KV, HD, SEQ).transpose(2, 0, 1)[None]

        return hid, to_cache(k_t), to_cache(v_t)

    return jax.shard_map(stage_program, mesh=mesh,
                         in_specs=(P('replica', None), P('replica'), gain_spec, spec_four, spec_four, spec_four, spec_four,
                                   gain_spec, spec_three, spec_three, spec_three),
                         out_specs=(P(('replica', 'stage'), None), P('stage', 'replica', None, None), P('stage', 'replica', None, None)),
                         check_vma=False)
```

time: 1600 us -> 592 us (0.37)
  waiting for transfers between devices: 727 us -> 0 us
  matrix products: 596 us -> 0 us
  Pallas kernels: 0 us -> 584 us
  other arithmetic: 149 us -> 0 us
  blocking collectives: 71.6 us -> 0 us
  local copies, waits for them, and re-layouts: 25.9 us -> 5.97 us
    ppermute x7 -> x0, waiting for transfers between devices: 727 us -> none  [tick_fn(): recv_buf = lax.ppermute(hidden_out, 'stage', send_pairs)]
    pallas_call x0 -> x1, Pallas kernels: none -> 584 us  [stage_program(): pl.pallas_call(stage_kernel, name='stage_pipeline', out_shape=(jax.ShapeD...]
    dot_general x36 -> x0, matrix products: 546 us -> none  [the longest x10 138 us: key_step(): jnp.einsum('hgqk,khd->hgqd', probs_blk.astype(jnp.bfloat16), value_blk, p...]
    reduce_sum x14 -> x0, other arithmetic: 110 us -> none  [the longest x10 103 us: key_step(): run_sum = run_sum * rescale + jnp.sum(probs_blk, axis=-1)]
    all_to_all x1 -> x0, blocking collectives: 71.6 us -> none  [stage_program(): delivered = lax.all_to_all(out_blocks, 'stage', 0, 0, tiled=True)]
    cond x12 -> x0, matrix products: 50.5 us -> none
    select_n x7 -> x0, other arithmetic: 22.1 us -> none  [tick_fn(): hidden_in = jnp.where(my_stage == 0, own_block, recv_buf)]
  transfers between devices with their start and end apart: 7 -> 0, of which waited for: 7 -> 0; matrix products, arithmetic and copies ran while one was open for 1% -> 0% of each run, Pallas kernels for 0% -> 0%
where the time goes in v1:
time: 592 us
  Pallas kernels  584 us (99%)
  local copies, waits for them, and re-layouts  5.97 us (1%)
    pallas_call x1, Pallas kernels, stage_program(): pl.pallas_call(stage_kernel, name='stage_pipeline', out_shape=(jax.ShapeD...  584 us

profile of v1, /device:TPU:7, one launch (start us, length us, event | category | flops | bytes accessed | tf_op | source)
XLA Modules:
  0.0 591.6 jit_solution(534253152248040050)
XLA Ops:
  1.3 584.3 %stage_pipeline.1 = (bf16[384,2048]{1,0:T(8,128)(2,1)}, bf16[512,1536]{1,0:T(8,128)(2,1)}, bf16[512,1536]{1,0:T(8,128)(2,1)}) custom-call(bf16[1536,2048]{1,0:T(8,128)(2,1)} %emb.1, s32[1]{0:T(128)S(6)} %copy.18.valid, f32[1,2048]{1,0:T(1,128)} %again.1, bf16[2048,2048]{1,0:T(8,128)(2,1)} %bitcast.32, bf16[512,2048]{1,0:T(8,128)(2,1)} %bitcast.34, ...), custom_call_target="tpu_custom_call" | custom-call | tf_op jit(solution)/shard_map/stage_pipeline/pallas_call | solution.py:395
  585.6 0.0 copy-start.1
  585.6 2.8 copy.19
  588.4 0.0 copy-done.1
  588.5 0.0 copy-start
  588.5 1.1 copy.20
  589.6 0.8 copy-done
  590.4 1.1 copy.21
Async XLA Ops:
  585.6 2.9 copy-start.1
  588.5 2.0 copy-start

commit v2 on v1

v2 whole, which is shorter than its diff:
```python
import math

import jax
import jax.numpy as jnp
import numpy as np
from jax import lax
from jax.experimental import pallas as pl
from jax.experimental.pallas import tpu as pltpu
from jax.sharding import PartitionSpec as P

EPS = 1e-5
ROPE_BASE = 10000.0
NEG = -1e30

SEQ = 1536
D = 2048
HEADS = 32
KV = 8
HD = 64
FF = 8192
STAGES = 4
B = 256
NB = SEQ // B
F = 512
NC = FF // F
NS = 3
VMIN = 768
VMAX = 1344
PIECE = SEQ // STAGES // 3
PER = B // PIECE
R = 4
SB = 2
AHEAD = 1
EXP_SCALE = math.log2(math.e)

F32 = jnp.float32
BF16 = jnp.bfloat16


def rope_tables():
    inv_freq = ROPE_BASE ** (-np.arange(HD // 2, dtype=np.float64) * (2.0 / HD))
    angles = inv_freq[:, None] * np.arange(SEQ, dtype=np.float64)[None, :]
    tab = np.zeros((NB, 2, HD // 2, 256), np.float32)
    for blk in range(NB):
        cols = slice(blk * B, (blk + 1) * B)
        tab[blk, 0, :, :B] = np.cos(angles[:, cols])
        tab[blk, 1, :, :B] = np.sin(angles[:, cols])
    return tab


def dot(a, b):
    return jnp.dot(a, b, preferred_element_type=F32)


def stage_kernel(emb, valid, again, wq, wk, wv, wo, mgain, wg, wu, wd, tab_hbm,
                 hid, kout, vout,
                 tab, wqkv_v, wo_v, wg_s, wu_s, wd_s, resid, kc, kst, vT, act, aT, qT, y, sbuf, mbuf, ff_s,
                 mask, vbias,
                 w_sem, tab_sem, g_sem, u_sem, d_sem, in_sem, send_sem, kv_sem, piece_sem, out_sem, credit):
    stage = lax.axis_index("stage")
    barrier = pltpu.get_barrier_semaphore()
    for k in range(1, STAGES):
        pl.semaphore_signal(barrier, inc=1, device_id={"stage": lax.rem(stage + k, STAGES)},
                            device_id_type=pl.DeviceIdType.MESH)

    def emb_copy(i):
        return pltpu.make_async_copy(emb.at[pl.ds(pl.multiple_of(i * B, B), B), :], resid.at[lax.rem(i, NS)], in_sem.at[lax.rem(i, NS)])

    def w_copy(p):
        if p < 4:
            src = wq.at[pl.ds(p * 512, 512), :]
        elif p == 4:
            src = wk
        elif p == 5:
            src = wv
        else:
            src = wo.at[pl.ds((p - 6) * 512, 512), :]
        dst = wqkv_v.at[pl.ds(p * 512, 512), :] if p < 6 else wo_v.at[pl.ds((p - 6) * 512, 512), :]
        return pltpu.make_async_copy(src, dst, w_sem.at[p])

    def gu_copy(c, s):
        cols = pl.ds(pl.multiple_of(c * F, F), F)
        return (pltpu.make_async_copy(wg.at[:, cols], wg_s[s], g_sem.at[s]),
                pltpu.make_async_copy(wu.at[:, cols], wu_s[s], u_sem.at[s]))

    def dn_copy(c, s):
        rows = pl.ds(pl.multiple_of(c * F, F), F)
        return pltpu.make_async_copy(wd.at[rows, :], wd_s[s], d_sem.at[s])

    tab_copy = pltpu.make_async_copy(tab_hbm, tab, tab_sem)

    @pl.when(stage == 0)
    def _():
        emb_copy(0).start()

    w_copy(0).start()
    tab_copy.start()
    for p in range(1, 10):
        w_copy(p).start()
    for c in range(R):
        for cp in gu_copy(c, c):
            cp.start()
        dn_copy(c, c).start()

    for g in range(KV):
        qT[g, pl.ds((1 - g % 2) * HD, HD), :] = jnp.zeros((HD, 4 * B), BF16)
    valid_pos = valid[0]
    vrow = lax.broadcasted_iota(jnp.int32, vbias.shape, 0) + VMIN
    vbias[...] = jnp.where(vrow < valid_pos, 0.0, NEG).astype(F32)
    tab_copy.wait()
    pl.semaphore_wait(barrier, STAGES - 1)

    def norm(slot, gain_ref):
        for r in range(0, B, 16):
            x = resid[slot, pl.ds(r, 16), :].astype(F32)
            inv = lax.rsqrt(jnp.mean(x * x, axis=-1, keepdims=True) + EPS)
            act[pl.ds(r, 16), :] = (x * inv * gain_ref[...]).astype(BF16)

    def rope(x, cos, sin):
        front = x[:HD // 2]
        back = x[HD // 2:]
        return front * cos - back * sin, back * cos + front * sin

    def project(i):
        for n in range(8):
            aT[pl.ds(n * 256, 256), :] = act[:, pl.ds(n * 256, 256)].T
        cos = tab[i, 0]
        sin = tab[i, 1]

        kt = dot(wqkv_v[pl.ds(2048, 512), :], aT[...])
        parts = []
        for h in range(KV):
            parts += list(rope(kt[h * HD:(h + 1) * HD], cos, sin))
        for half in range(2):
            kh = jnp.concatenate(parts[half * 8:half * 8 + 8], axis=0).astype(BF16)
            kst[pl.ds(half * 256, 256), :] = kh
            kc[pl.ds(pl.multiple_of(i * B, B), B), pl.ds(half * 256, 256)] = kh.T
        vt = dot(wqkv_v[pl.ds(2560, 512), :], aT[...])
        vT[:, pl.ds(pl.multiple_of(i * B, B), B)] = vt.astype(BF16)

        for pair in range(4):
            qt = dot(wqkv_v[pl.ds(pair * 512, 512), :], aT[...])
            for h in range(8):
                f, b = rope(qt[h * HD:(h + 1) * HD], cos, sin)
                g = pair * 2 + h // 4
                row = (g % 2) * HD
                cols = pl.ds((h % 4) * B, B)
                qT[g, pl.ds(row, HD // 2), cols] = (f * 0.125).astype(BF16)
                qT[g, pl.ds(row + HD // 2, HD // 2), cols] = (b * 0.125).astype(BF16)

    def make_mask(i):
        key = lax.broadcasted_iota(jnp.int32, (B, B), 0)
        tok = lax.broadcasted_iota(jnp.int32, (B, B), 1)
        ok = (key <= tok) & (key + i * B < valid_pos)
        mask[...] = jnp.where(ok, 0.0, NEG).astype(F32)

    def attend(n):
        spans = [(c * B, min(B, VMAX - c * B)) for c in range(n + 1)]
        total = spans[-1][0] + spans[-1][1]

        def sbuffer(u):
            return y if u % SB == 0 else sbuf.at[u % SB - 1]

        def scores(g, u):
            sref = sbuffer(u)
            kcols = pl.ds(pl.multiple_of((g // 2) * 128, 128), 128)
            q = qT[g, :, pl.ds((u % 4) * B, B)]
            m = None
            for start, rows in spans:
                s = dot(kc[pl.ds(start, rows), kcols], q)
                if start == n * B:
                    s = s + mask[pl.ds(0, rows), :]
                elif start >= VMIN:
                    mk = vbias[pl.ds(start - VMIN, rows), :]
                    s = s + jnp.concatenate([mk, mk], axis=1)
                sref[pl.ds(start, rows), :] = s
                cm = jnp.max(s.reshape(rows // 8, 8, B), axis=0)
                m = cm if m is None else jnp.maximum(m, cm)
            mbuf[u % SB] = m

        def weighted(g, u):
            sref = sbuffer(u)
            mc = jnp.max(mbuf[u % SB], axis=0, keepdims=True) * EXP_SCALE
            l = None
            probs = []
            for start, rows in spans:
                p = jnp.exp2(sref[pl.ds(start, rows), :] * EXP_SCALE - mc)
                ls = jnp.sum(p.reshape(rows // 8, 8, B), axis=0)
                l = ls if l is None else l + ls
                probs.append(p.astype(BF16))
            o = dot(vT[pl.ds(pl.multiple_of(g * HD, HD), HD), pl.ds(0, total)], jnp.concatenate(probs, axis=0))
            return (o * (1.0 / jnp.sum(l, axis=0, keepdims=True))).astype(BF16)

        for u in range(AHEAD):
            scores(0, u)

        def group_pair(pair, _):
            g = pair * 2
            g_next = lax.rem(g + 2, KV)
            outs = []
            for u in range(8):
                ahead = u + AHEAD
                scores(g + ahead // 4 if ahead < 8 else g_next, ahead)
                outs.append(weighted(g + u // 4, u))
                if u % 4 == 3:
                    act[:, pl.ds(pl.multiple_of((g + u // 4) * 256, 256), 256)] = jnp.concatenate(outs, axis=0).T
                    outs = []
            return 0

        lax.fori_loop(0, KV // 2, group_pair, 0)

    def out_proj(slot):
        for n in range(4):
            cols = pl.ds(n * 512, 512)
            o = dot(act[pl.ds(0, B), :], wo_v[:, cols])
            resid[slot, :, cols] = (resid[slot, :, cols].astype(F32) + o).astype(BF16)

    def gate_up(s):
        x = act[pl.ds(0, B), :]
        gate = dot(x, wg_s[s][...])
        up = dot(x, wu_s[s][...])
        ff_s[s % 2][...] = (gate * jax.nn.sigmoid(gate) * up).astype(BF16)

    def down(s):
        x = ff_s[s % 2][...]
        for n in range(8):
            rows = pl.ds(n * B, B)
            y[rows, :] = y[rows, :] + dot(x, wd_s[s][:, pl.ds(n * 256, 256)])

    def wait_gu(s):
        for cp in gu_copy(0, s):
            cp.wait()

    def wait_dn(s):
        dn_copy(0, s).wait()

    def start_gu(c, s, ok):
        @pl.when(ok)
        def _():
            for cp in gu_copy(lax.rem(c, NC), s):
                cp.start()

    def start_dn(c, s, ok):
        @pl.when(ok)
        def _():
            dn_copy(lax.rem(c, NC), s).start()

    def mlp(i, slot):
        for n in range(8):
            y[pl.ds(n * B, B), :] = resid[slot, :, pl.ds(n * 256, 256)].astype(F32)
        more = i + 1 < NB
        wait_gu(0)
        gate_up(0)
        start_gu(R, 0, True)

        def steps(it, _):
            c = it * R
            for u in range(R):
                if u % 2 == 0:
                    wait_gu((u + 1) % R)
                    wait_gu((u + 2) % R)
                    wait_dn(u)
                    wait_dn(u + 1)
                gate_up((u + 1) % R)
                start_gu(c + u + 1 + R, (u + 1) % R, more | (c + u + 1 + R < NC))
                down(u)
                start_dn(c + u + R, u, more | (c + u + R < NC))
            return 0

        lax.fori_loop(0, NC // R - 1, steps, 0)
        for u in range(R):
            if u % 2 == 0:
                wait_gu(u + 1)
                if u + 2 < R:
                    wait_gu(u + 2)
                wait_dn(u)
                wait_dn(u + 1)
            if u + 1 < R:
                gate_up(u + 1)
                start_gu(u + 1, u + 1, more)
            down(u)
            start_dn(u, u, more)
        for n in range(8):
            resid[slot, :, pl.ds(n * 256, 256)] = y[pl.ds(n * B, B), :].astype(BF16)

    def next_copy(i):
        slot = lax.rem(i, NS)
        return pltpu.make_async_remote_copy(resid.at[slot], resid.at[slot], send_sem.at[slot], in_sem.at[slot],
                                            device_id={"stage": lax.rem(stage + 1, STAGES)},
                                            device_id_type=pl.DeviceIdType.MESH)

    def piece_copy(i, r):
        slot = lax.rem(i, NS)
        piece = i * PER + r
        row = lax.rem(piece, 3)
        src = resid.at[slot, pl.ds(r * PIECE, PIECE), :]
        dst = hid.at[pl.ds(pl.multiple_of(row * PIECE, PIECE), PIECE), :]
        remote = pltpu.make_async_remote_copy(src, dst, piece_sem.at[slot, r], out_sem.at[row],
                                              device_id={"stage": piece // 3}, device_id_type=pl.DeviceIdType.MESH)
        return remote, pltpu.make_async_copy(src, dst, out_sem.at[row]), piece // 3 == STAGES - 1

    def k_copy(i):
        cols = pl.ds(pl.multiple_of(i * B, B), B)
        return pltpu.make_async_copy(kst, kout.at[:, cols], kv_sem.at[0])

    def v_copy(i):
        cols = pl.ds(pl.multiple_of(i * B, B), B)
        return pltpu.make_async_copy(vT.at[:, cols], vout.at[:, cols], kv_sem.at[1])

    last = stage == STAGES - 1

    def block(i, _):
        slot = lax.rem(i, NS)
        emb_copy(i).wait()

        @pl.when((stage == 0) & (i + 1 < NB))
        def _():
            emb_copy(i + 1).start()

        @pl.when(i > 0)
        def _():
            k_copy(0).wait()
            v_copy(0).wait()

        norm(slot, again)

        @pl.when(i == 0)
        def _():
            for p in range(6):
                w_copy(p).wait()

        project(i)
        make_mask(i)
        for n in range(NB):
            @pl.when(i == n)
            def _():
                attend(n)

        @pl.when(i == 0)
        def _():
            for p in range(6, 10):
                w_copy(p).wait()

        out_proj(slot)
        norm(slot, mgain)
        mlp(i, slot)

        k_copy(i).start()
        v_copy(i).start()

        @pl.when(jnp.logical_not(last) & (i >= NS))
        def _():
            pl.semaphore_wait(credit, 1)

        @pl.when(jnp.logical_not(last))
        def _():
            next_copy(i).start()

        for r in range(PER):
            remote, local, mine = piece_copy(i, r)

            @pl.when(last & jnp.logical_not(mine))
            def _():
                remote.start()

            @pl.when(last & mine)
            def _():
                local.start()

        @pl.when((i >= 1) & jnp.logical_not(last))
        def _():
            next_copy(i - 1).wait_send()

        for r in range(PER):
            remote, local, mine = piece_copy(i - 1, r)

            @pl.when((i >= 1) & last & jnp.logical_not(mine))
            def _():
                remote.wait_send()

        @pl.when((stage > 0) & (i >= 1) & (i - 1 + NS < NB))
        def _():
            pl.semaphore_signal(credit, inc=1, device_id={"stage": lax.rem(stage + STAGES - 1, STAGES)},
                                device_id_type=pl.DeviceIdType.MESH)

        return 0

    lax.fori_loop(0, NB, block, 0)

    @pl.when(jnp.logical_not(last))
    def _():
        next_copy(NB - 1).wait_send()

    for row in range(3):
        piece_copy(row // PER, row % PER)[1].wait()
    k_copy(0).wait()
    v_copy(0).wait()


def solution(mesh):
    gain_spec = P('stage', None)
    spec_three = P('stage', None, None)
    spec_four = P('stage', None, None, None)
    table = rope_tables()
    dma = pltpu.SemaphoreType.DMA

    def stage_program(embeddings, valid_len, attn_gain, w_q, w_k, w_v, w_o, mlp_gain, w_gate, w_up, w_down):
        wq = w_q[0].transpose(1, 2, 0).reshape(HEADS * HD, D)
        wk = w_k[0].transpose(1, 2, 0).reshape(KV * HD, D)
        wv = w_v[0].transpose(1, 2, 0).reshape(KV * HD, D)
        wo = w_o[0].reshape(HEADS * HD, D)
        any_spec = pl.BlockSpec(memory_space=pl.ANY)
        vmem_spec = pl.BlockSpec(memory_space=pltpu.VMEM)
        smem_spec = pl.BlockSpec(memory_space=pltpu.SMEM)
        hid, k_t, v_t = pl.pallas_call(
            stage_kernel,
            name="stage_pipeline",
            out_shape=(jax.ShapeDtypeStruct((SEQ // STAGES, D), BF16),
                       jax.ShapeDtypeStruct((KV * HD, SEQ), BF16),
                       jax.ShapeDtypeStruct((KV * HD, SEQ), BF16)),
            in_specs=[any_spec, smem_spec, vmem_spec, any_spec, any_spec, any_spec, any_spec, vmem_spec,
                      any_spec, any_spec, any_spec, any_spec],
            out_specs=(any_spec, any_spec, any_spec),
            scratch_shapes=[
                pltpu.VMEM((NB, 2, HD // 2, 256), F32),
                pltpu.VMEM((3072, D), BF16),
                pltpu.VMEM((D, D), BF16),
                [pltpu.VMEM((D, F), BF16)] * R,
                [pltpu.VMEM((D, F), BF16)] * R,
                [pltpu.VMEM((F, D), BF16)] * R,
                pltpu.VMEM((NS, B, D), BF16),
                pltpu.VMEM((SEQ, KV * HD), BF16),
                pltpu.VMEM((KV * HD, B), BF16),
                pltpu.VMEM((KV * HD, SEQ), BF16),
                pltpu.VMEM((256, D), BF16),
                pltpu.VMEM((D, 256), BF16),
                pltpu.VMEM((KV, 2 * HD, 4 * B), BF16),
                pltpu.VMEM((8 * B, 256), F32),
                pltpu.VMEM((SB - 1, VMAX, B), F32),
                pltpu.VMEM((SB, 8, B), F32),
                [pltpu.VMEM((B, F), BF16)] * 2,
                pltpu.VMEM((B, B), F32),
                pltpu.VMEM((VMAX - VMIN, 128), F32),
                dma((10,)), dma, dma((R,)), dma((R,)), dma((R,)), dma((NS,)), dma((NS,)), dma((2,)), dma((NS, PER)), dma((3,)),
                pltpu.SemaphoreType.REGULAR,
            ],
            compiler_params=pltpu.CompilerParams(collective_id=0, has_side_effects=True,
                                                 vmem_limit_bytes=67043328),
        )(embeddings, valid_len, attn_gain, wq, wk, wv, wo, mlp_gain, w_gate[0], w_up[0], w_down[0],
          jnp.asarray(table))

        def to_cache(x):
            return x.reshape(KV, HD, SEQ).transpose(2, 0, 1)[None]

        return hid, to_cache(k_t), to_cache(v_t)

    return jax.shard_map(stage_program, mesh=mesh,
                         in_specs=(P('replica', None), P('replica'), gain_spec, spec_four, spec_four, spec_four, spec_four,
                                   gain_spec, spec_three, spec_three, spec_three),
                         out_specs=(P(('replica', 'stage'), None), P('stage', 'replica', None, None), P('stage', 'replica', None, None)),
                         check_vma=False)
```

time: 592 us -> 446 us (0.75)
  Pallas kernels: 584 us -> 439 us
    pallas_call x1, Pallas kernels: 584 us -> 439 us  [stage_program(): pl.pallas_call(stage_kernel, name='stage_pipeline', out_shape=(jax.ShapeD...]
where the time goes in v2:
time: 446 us
  Pallas kernels  439 us (98%)
  local copies, waits for them, and re-layouts  5.97 us (1%)
    pallas_call x1, Pallas kernels, stage_program(): pl.pallas_call(stage_kernel, name='stage_pipeline', out_shape=(jax.ShapeD...  439 us

profile of v2, /device:TPU:7, one launch (start us, length us, event | category | flops | bytes accessed | tf_op | source)
XLA Modules:
  0.0 445.8 jit_solution(11278113411289293950)
XLA Ops:
  1.3 438.5 %stage_pipeline.1 = (bf16[384,2048]{1,0:T(8,128)(2,1)}, bf16[512,1536]{1,0:T(8,128)(2,1)}, bf16[512,1536]{1,0:T(8,128)(2,1)}) custom-call(bf16[1536,2048]{1,0:T(8,128)(2,1)} %emb.1, s32[1]{0:T(128)S(6)} %copy.18.valid, f32[1,2048]{1,0:T(1,128)} %again.1, bf16[2048,2048]{1,0:T(8,128)(2,1)} %bitcast.32, bf16[512,2048]{1,0:T(8,128)(2,1)} %bitcast.34, ...), custom_call_target="tpu_custom_call" | custom-call | tf_op jit(solution)/shard_map/stage_pipeline/pallas_call | solution.py:415
  439.8 0.0 copy-start.1
  439.8 2.8 copy.19
  442.7 0.0 copy-done.1
  442.7 0.0 copy-start
  442.7 1.1 copy.20
  443.8 0.8 copy-done
  444.6 1.1 copy.21
Async XLA Ops:
  439.8 2.9 copy-start.1
  442.7 2.0 copy-start

commit v3 on v2

--- a/solution.py
+++ b/solution.py
@@ -29,8 +29,8 @@
 PIECE = SEQ // STAGES // 3
 PER = B // PIECE
 R = 4
-SB = 2
-AHEAD = 1
+SB = 4
+AHEAD = 2
 EXP_SCALE = math.log2(math.e)
 
 F32 = jnp.float32
@@ -52,9 +52,13 @@
     return jnp.dot(a, b, preferred_element_type=F32)
 
 
+def dot_t(a, b):
+    return lax.dot_general(a, b, (((1,), (1,)), ((), ())), preferred_element_type=F32)
+
+
 def stage_kernel(emb, valid, again, wq, wk, wv, wo, mgain, wg, wu, wd, tab_hbm,
                  hid, kout, vout,
-                 tab, wqkv_v, wo_v, wg_s, wu_s, wd_s, resid, kc, kst, vT, act, aT, qT, y, sbuf, mbuf, ff_s,
+                 tab, wqkv_v, wo_v, wg_s, wu_s, wd_s, resid, kc, vT, act, qT, y, mbuf, ff_s,
                  mask, vbias,
                  w_sem, tab_sem, g_sem, u_sem, d_sem, in_sem, send_sem, kv_sem, piece_sem, out_sem, credit):
     stage = lax.axis_index("stage")
@@ -93,9 +97,9 @@
     def _():
         emb_copy(0).start()
 
-    w_copy(0).start()
+    w_copy(4).start()
     tab_copy.start()
-    for p in range(1, 10):
+    for p in (5, 0, 1, 2, 3, 6, 7, 8, 9):
         w_copy(p).start()
     for c in range(R):
         for cp in gu_copy(c, c):
@@ -107,8 +111,6 @@
     valid_pos = valid[0]
     vrow = lax.broadcasted_iota(jnp.int32, vbias.shape, 0) + VMIN
     vbias[...] = jnp.where(vrow < valid_pos, 0.0, NEG).astype(F32)
-    tab_copy.wait()
-    pl.semaphore_wait(barrier, STAGES - 1)
 
     def norm(slot, gain_ref):
         for r in range(0, B, 16):
@@ -122,24 +124,22 @@
         return front * cos - back * sin, back * cos + front * sin
 
     def project(i):
-        for n in range(8):
-            aT[pl.ds(n * 256, 256), :] = act[:, pl.ds(n * 256, 256)].T
         cos = tab[i, 0]
         sin = tab[i, 1]
 
-        kt = dot(wqkv_v[pl.ds(2048, 512), :], aT[...])
+        kt = dot_t(wqkv_v[pl.ds(2048, 512), :], act[...])
         parts = []
         for h in range(KV):
             parts += list(rope(kt[h * HD:(h + 1) * HD], cos, sin))
         for half in range(2):
             kh = jnp.concatenate(parts[half * 8:half * 8 + 8], axis=0).astype(BF16)
-            kst[pl.ds(half * 256, 256), :] = kh
+            ff_s[1][:, pl.ds(half * 256, 256)] = kh
             kc[pl.ds(pl.multiple_of(i * B, B), B), pl.ds(half * 256, 256)] = kh.T
-        vt = dot(wqkv_v[pl.ds(2560, 512), :], aT[...])
+        vt = dot_t(wqkv_v[pl.ds(2560, 512), :], act[...])
         vT[:, pl.ds(pl.multiple_of(i * B, B), B)] = vt.astype(BF16)
 
         for pair in range(4):
-            qt = dot(wqkv_v[pl.ds(pair * 512, 512), :], aT[...])
+            qt = dot_t(wqkv_v[pl.ds(pair * 512, 512), :], act[...])
             for h in range(8):
                 f, b = rope(qt[h * HD:(h + 1) * HD], cos, sin)
                 g = pair * 2 + h // 4
@@ -158,11 +158,7 @@
         spans = [(c * B, min(B, VMAX - c * B)) for c in range(n + 1)]
         total = spans[-1][0] + spans[-1][1]
 
-        def sbuffer(u):
-            return y if u % SB == 0 else sbuf.at[u % SB - 1]
-
         def scores(g, u):
-            sref = sbuffer(u)
             kcols = pl.ds(pl.multiple_of((g // 2) * 128, 128), 128)
             q = qT[g, :, pl.ds((u % 4) * B, B)]
             m = None
@@ -173,18 +169,17 @@
                 elif start >= VMIN:
                     mk = vbias[pl.ds(start - VMIN, rows), :]
                     s = s + jnp.concatenate([mk, mk], axis=1)
-                sref[pl.ds(start, rows), :] = s
+                y[pl.ds((u % SB) * total + start, rows), :] = s
                 cm = jnp.max(s.reshape(rows // 8, 8, B), axis=0)
                 m = cm if m is None else jnp.maximum(m, cm)
             mbuf[u % SB] = m
 
         def weighted(g, u):
-            sref = sbuffer(u)
             mc = jnp.max(mbuf[u % SB], axis=0, keepdims=True) * EXP_SCALE
             l = None
             probs = []
             for start, rows in spans:
-                p = jnp.exp2(sref[pl.ds(start, rows), :] * EXP_SCALE - mc)
+                p = jnp.exp2(y[pl.ds((u % SB) * total + start, rows), :] * EXP_SCALE - mc)
                 ls = jnp.sum(p.reshape(rows // 8, 8, B), axis=0)
                 l = ls if l is None else l + ls
                 probs.append(p.astype(BF16))
@@ -196,11 +191,10 @@
 
         def group_pair(pair, _):
             g = pair * 2
-            g_next = lax.rem(g + 2, KV)
             outs = []
             for u in range(8):
                 ahead = u + AHEAD
-                scores(g + ahead // 4 if ahead < 8 else g_next, ahead)
+                scores(g + ahead // 4 if ahead < 8 else lax.rem(g + 2, KV), ahead)
                 outs.append(weighted(g + u // 4, u))
                 if u % 4 == 3:
                     act[:, pl.ds(pl.multiple_of((g + u // 4) * 256, 256), 256)] = jnp.concatenate(outs, axis=0).T
@@ -249,37 +243,37 @@
         for n in range(8):
             y[pl.ds(n * B, B), :] = resid[slot, :, pl.ds(n * 256, 256)].astype(F32)
         more = i + 1 < NB
-        wait_gu(0)
-        gate_up(0)
-        start_gu(R, 0, True)
 
         def steps(it, _):
-            c = it * R
-            for u in range(R):
-                if u % 2 == 0:
-                    wait_gu((u + 1) % R)
-                    wait_gu((u + 2) % R)
-                    wait_dn(u)
-                    wait_dn(u + 1)
-                gate_up((u + 1) % R)
-                start_gu(c + u + 1 + R, (u + 1) % R, more | (c + u + 1 + R < NC))
-                down(u)
-                start_dn(c + u + R, u, more | (c + u + R < NC))
+            again_ok = more | (it < NC // R - 1)
+            c = (it + 1) * R
+            wait_gu(0)
+            wait_gu(1)
+            wait_dn(0)
+            gate_up(0)
+            start_gu(c, 0, again_ok)
+            gate_up(1)
+            start_gu(c + 1, 1, again_ok)
+            down(0)
+            start_dn(c, 0, again_ok)
+            wait_gu(2)
+            wait_dn(1)
+            gate_up(2)
+            start_gu(c + 2, 2, again_ok)
+            down(1)
+            start_dn(c + 1, 1, again_ok)
+            wait_gu(3)
+            wait_dn(2)
+            wait_dn(3)
+            gate_up(3)
+            start_gu(c + 3, 3, again_ok)
+            down(2)
+            start_dn(c + 2, 2, again_ok)
+            down(3)
+            start_dn(c + 3, 3, again_ok)
             return 0
 
-        lax.fori_loop(0, NC // R - 1, steps, 0)
-        for u in range(R):
-            if u % 2 == 0:
-                wait_gu(u + 1)
-                if u + 2 < R:
-                    wait_gu(u + 2)
-                wait_dn(u)
-                wait_dn(u + 1)
-            if u + 1 < R:
-                gate_up(u + 1)
-                start_gu(u + 1, u + 1, more)
-            down(u)
-            start_dn(u, u, more)
+        lax.fori_loop(0, NC // R, steps, 0)
         for n in range(8):
             resid[slot, :, pl.ds(n * 256, 256)] = y[pl.ds(n * B, B), :].astype(BF16)
 
@@ -299,13 +293,14 @@
                                               device_id={"stage": piece // 3}, device_id_type=pl.DeviceIdType.MESH)
         return remote, pltpu.make_async_copy(src, dst, out_sem.at[row]), piece // 3 == STAGES - 1
 
-    def k_copy(i):
+    def k_copy(i, half):
         cols = pl.ds(pl.multiple_of(i * B, B), B)
-        return pltpu.make_async_copy(kst, kout.at[:, cols], kv_sem.at[0])
+        return pltpu.make_async_copy(ff_s[1].at[:, pl.ds(half * 256, 256)], kout.at[pl.ds(half * 256, 256), cols],
+                                     kv_sem.at[half])
 
     def v_copy(i):
         cols = pl.ds(pl.multiple_of(i * B, B), B)
-        return pltpu.make_async_copy(vT.at[:, cols], vout.at[:, cols], kv_sem.at[1])
+        return pltpu.make_async_copy(vT.at[:, cols], vout.at[:, cols], kv_sem.at[2])
 
     last = stage == STAGES - 1
 
@@ -313,24 +308,19 @@
         slot = lax.rem(i, NS)
         emb_copy(i).wait()
 
-        @pl.when((stage == 0) & (i + 1 < NB))
-        def _():
-            emb_copy(i + 1).start()
-
-        @pl.when(i > 0)
-        def _():
-            k_copy(0).wait()
-            v_copy(0).wait()
-
         norm(slot, again)
 
         @pl.when(i == 0)
         def _():
+            tab_copy.wait()
             for p in range(6):
                 w_copy(p).wait()
 
         project(i)
         make_mask(i)
+        k_copy(i, 0).start()
+        k_copy(i, 1).start()
+        v_copy(i).start()
         for n in range(NB):
             @pl.when(i == n)
             def _():
@@ -338,15 +328,41 @@
 
         @pl.when(i == 0)
         def _():
+            pl.semaphore_wait(barrier, STAGES - 1)
+
+        @pl.when((i >= 1) & jnp.logical_not(last))
+        def _():
+            next_copy(i - 1).wait_send()
+
+        for r in range(PER):
+            remote, local, mine = piece_copy(i - 1, r)
+
+            @pl.when((i >= 1) & last & jnp.logical_not(mine))
+            def _():
+                remote.wait_send()
+
+        @pl.when((stage > 0) & (i >= 1) & (i - 1 + NS < NB))
+        def _():
+            pl.semaphore_signal(credit, inc=1, device_id={"stage": lax.rem(stage + STAGES - 1, STAGES)},
+                                device_id_type=pl.DeviceIdType.MESH)
+
+        @pl.when((stage == 0) & (i + 1 < NB))
+        def _():
+            emb_copy(i + 1).start()
+
+
+        @pl.when(i == 0)
+        def _():
             for p in range(6, 10):
                 w_copy(p).wait()
 
+        k_copy(i, 0).wait()
+        k_copy(i, 1).wait()
+        v_copy(i).wait()
         out_proj(slot)
         norm(slot, mgain)
         mlp(i, slot)
 
-        k_copy(i).start()
-        v_copy(i).start()
 
         @pl.when(jnp.logical_not(last) & (i >= NS))
         def _():
@@ -367,22 +383,6 @@
             def _():
                 local.start()
 
-        @pl.when((i >= 1) & jnp.logical_not(last))
-        def _():
-            next_copy(i - 1).wait_send()
-
-        for r in range(PER):
-            remote, local, mine = piece_copy(i - 1, r)
-
-            @pl.when((i >= 1) & last & jnp.logical_not(mine))
-            def _():
-                remote.wait_send()
-
-        @pl.when((stage > 0) & (i >= 1) & (i - 1 + NS < NB))
-        def _():
-            pl.semaphore_signal(credit, inc=1, device_id={"stage": lax.rem(stage + STAGES - 1, STAGES)},
-                                device_id_type=pl.DeviceIdType.MESH)
-
         return 0
 
     lax.fori_loop(0, NB, block, 0)
@@ -393,9 +393,6 @@
 
     for row in range(3):
         piece_copy(row // PER, row % PER)[1].wait()
-    k_copy(0).wait()
-    v_copy(0).wait()
-
 
 def solution(mesh):
     gain_spec = P('stage', None)
@@ -430,18 +427,15 @@
                 [pltpu.VMEM((F, D), BF16)] * R,
                 pltpu.VMEM((NS, B, D), BF16),
                 pltpu.VMEM((SEQ, KV * HD), BF16),
-                pltpu.VMEM((KV * HD, B), BF16),
                 pltpu.VMEM((KV * HD, SEQ), BF16),
                 pltpu.VMEM((256, D), BF16),
-                pltpu.VMEM((D, 256), BF16),
                 pltpu.VMEM((KV, 2 * HD, 4 * B), BF16),
-                pltpu.VMEM((8 * B, 256), F32),
-                pltpu.VMEM((SB - 1, VMAX, B), F32),
+                pltpu.VMEM((SB * VMAX, B), F32),
                 pltpu.VMEM((SB, 8, B), F32),
                 [pltpu.VMEM((B, F), BF16)] * 2,
                 pltpu.VMEM((B, B), F32),
                 pltpu.VMEM((VMAX - VMIN, 128), F32),
-                dma((10,)), dma, dma((R,)), dma((R,)), dma((R,)), dma((NS,)), dma((NS,)), dma((2,)), dma((NS, PER)), dma((3,)),
+                dma((10,)), dma, dma((R,)), dma((R,)), dma((R,)), dma((NS,)), dma((NS,)), dma((3,)), dma((NS, PER)), dma((3,)),
                 pltpu.SemaphoreType.REGULAR,
             ],
             compiler_params=pltpu.CompilerParams(collective_id=0, has_side_effects=True,

time: 446 us -> 447 us (level)
  no operation moved by 1% of the time
where the time goes in v3:
time: 447 us
  Pallas kernels  440 us (98%)
  local copies, waits for them, and re-layouts  5.97 us (1%)
    pallas_call x1, Pallas kernels, stage_program(): pl.pallas_call(stage_kernel, name='stage_pipeline', out_shape=(jax.ShapeD...  440 us

profile of v3, /device:TPU:7, one launch (start us, length us, event | category | flops | bytes accessed | tf_op | source)
XLA Modules:
  0.0 446.8 jit_solution(6641796506077524223)
XLA Ops:
  1.3 439.6 %stage_pipeline.1 = (bf16[384,2048]{1,0:T(8,128)(2,1)}, bf16[512,1536]{1,0:T(8,128)(2,1)}, bf16[512,1536]{1,0:T(8,128)(2,1)}) custom-call(bf16[1536,2048]{1,0:T(8,128)(2,1)} %emb.1, s32[1]{0:T(128)S(6)} %copy.18.valid, f32[1,2048]{1,0:T(1,128)} %again.1, bf16[2048,2048]{1,0:T(8,128)(2,1)} %bitcast.32, bf16[512,2048]{1,0:T(8,128)(2,1)} %bitcast.34, ...), custom_call_target="tpu_custom_call" | custom-call | tf_op jit(solution)/shard_map/stage_pipeline/pallas_call | solution.py:412
  440.9 0.0 copy-start.1
  440.9 2.8 copy.19
  443.7 0.0 copy-done.1
  443.7 0.0 copy-start
  443.7 1.1 copy.20
  444.9 0.8 copy-done
  445.7 1.1 copy.21
Async XLA Ops:
  440.9 2.9 copy-start.1
  443.7 2.0 copy-start

commit v4 on v3

--- a/solution.py
+++ b/solution.py
@@ -30,7 +30,6 @@
 PER = B // PIECE
 R = 4
 SB = 4
-AHEAD = 2
 EXP_SCALE = math.log2(math.e)
 
 F32 = jnp.float32
@@ -56,10 +55,10 @@
     return lax.dot_general(a, b, (((1,), (1,)), ((), ())), preferred_element_type=F32)
 
 
-def stage_kernel(emb, valid, again, wq, wk, wv, wo, mgain, wg, wu, wd, tab_hbm,
+def stage_kernel(emb, valid, again_hbm, wq, wk, wv, wo, mgain_hbm, wg, wu, wd, tab_hbm,
                  hid, kout, vout,
-                 tab, wqkv_v, wo_v, wg_s, wu_s, wd_s, resid, kc, vT, act, qT, y, mbuf, ff_s,
-                 mask, vbias,
+                 tab, again, mgain, wqkv_v, wo_v, wg_s, wu_s, wd_s, resid, kc, vT, act, qT, y, mbuf, ff_s,
+                 mask, vbias, kbias, qones,
                  w_sem, tab_sem, g_sem, u_sem, d_sem, in_sem, send_sem, kv_sem, piece_sem, out_sem, credit):
     stage = lax.axis_index("stage")
     barrier = pltpu.get_barrier_semaphore()
@@ -91,26 +90,28 @@
         rows = pl.ds(pl.multiple_of(c * F, F), F)
         return pltpu.make_async_copy(wd.at[rows, :], wd_s[s], d_sem.at[s])
 
-    tab_copy = pltpu.make_async_copy(tab_hbm, tab, tab_sem)
+    small_copies = [pltpu.make_async_copy(src, dst, tab_sem.at[n])
+                    for n, (src, dst) in enumerate(((again_hbm, again), (mgain_hbm, mgain), (tab_hbm, tab)))]
 
     @pl.when(stage == 0)
     def _():
         emb_copy(0).start()
 
-    w_copy(4).start()
-    tab_copy.start()
-    for p in (5, 0, 1, 2, 3, 6, 7, 8, 9):
+    for cp in small_copies:
+        cp.start()
+    for p in range(6):
         w_copy(p).start()
-    for c in range(R):
-        for cp in gu_copy(c, c):
-            cp.start()
-        dn_copy(c, c).start()
 
     for g in range(KV):
         qT[g, pl.ds((1 - g % 2) * HD, HD), :] = jnp.zeros((HD, 4 * B), BF16)
     valid_pos = valid[0]
-    vrow = lax.broadcasted_iota(jnp.int32, vbias.shape, 0) + VMIN
-    vbias[...] = jnp.where(vrow < valid_pos, 0.0, NEG).astype(F32)
+    row = lax.broadcasted_iota(jnp.int32, vbias.shape, 0) + VMIN
+    vbias[...] = jnp.where(row < valid_pos, 0.0, NEG).astype(F32)
+    row = lax.broadcasted_iota(jnp.int32, kbias.shape, 0) + VMIN
+    lane = lax.broadcasted_iota(jnp.int32, kbias.shape, 1)
+    kbias[...] = jnp.where((lane == 0) & (row >= valid_pos), NEG, 0.0).astype(BF16)
+    row = lax.broadcasted_iota(jnp.int32, qones.shape, 0)
+    qones[...] = jnp.where(row == 0, 1.0, 0.0).astype(BF16)
 
     def norm(slot, gain_ref):
         for r in range(0, B, 16):
@@ -149,51 +150,70 @@
                 qT[g, pl.ds(row + HD // 2, HD // 2), cols] = (b * 0.125).astype(BF16)
 
     def make_mask(i):
-        key = lax.broadcasted_iota(jnp.int32, (B, B), 0)
-        tok = lax.broadcasted_iota(jnp.int32, (B, B), 1)
+        key = lax.broadcasted_iota(jnp.int32, mask.shape, 0)
+        tok = lax.broadcasted_iota(jnp.int32, mask.shape, 1)
+        key = jnp.where(tok < B, key, key + B // 2)
+        tok = jnp.where(tok < B, tok, tok - B // 2)
         ok = (key <= tok) & (key + i * B < valid_pos)
         mask[...] = jnp.where(ok, 0.0, NEG).astype(F32)
 
     def attend(n):
-        spans = [(c * B, min(B, VMAX - c * B)) for c in range(n + 1)]
+        spans = [(c * B, min(B, VMAX - c * B), 0) for c in range(n + 1)]
+        if spans[-1][1] == B:
+            spans[-1:] = [(n * B, B // 2, 0), (n * B + B // 2, B // 2, B // 2)]
         total = spans[-1][0] + spans[-1][1]
+        ahead_by = 1 if n == NB - 2 else 2
 
         def scores(g, u):
             kcols = pl.ds(pl.multiple_of((g // 2) * 128, 128), 128)
             q = qT[g, :, pl.ds((u % 4) * B, B)]
             m = None
-            for start, rows in spans:
-                s = dot(kc[pl.ds(start, rows), kcols], q)
-                if start == n * B:
-                    s = s + mask[pl.ds(0, rows), :]
+            for start, rows, lane in spans:
+                keys = kc[pl.ds(start, rows), kcols]
+                if start >= n * B:
+                    s = dot(keys, q[:, lane:]) + mask[pl.ds(0, rows), pl.ds(2 * lane, B - lane)]
+                elif start >= VMIN and n == NB - 1:
+                    bias = vbias[pl.ds(start - VMIN, rows), :]
+                    s = dot(keys, q) + jnp.concatenate([bias, bias], axis=1)
                 elif start >= VMIN:
-                    mk = vbias[pl.ds(start - VMIN, rows), :]
-                    s = s + jnp.concatenate([mk, mk], axis=1)
-                y[pl.ds((u % SB) * total + start, rows), :] = s
-                cm = jnp.max(s.reshape(rows // 8, 8, B), axis=0)
-                m = cm if m is None else jnp.maximum(m, cm)
+                    bias = kbias[pl.ds(start - VMIN, rows), :]
+                    s = dot(jnp.concatenate([keys, bias], axis=1), jnp.concatenate([q, qones[...]], axis=0))
+                else:
+                    s = dot(keys, q)
+                y[pl.ds((u % SB) * total + start, rows), pl.ds(lane, B - lane)] = s
+                cm = jnp.max(s.reshape(rows // 8, 8, B - lane), axis=0)
+                if lane:
+                    m = jnp.concatenate([m[:, :lane], jnp.maximum(m[:, lane:], cm)], axis=1)
+                else:
+                    m = cm if m is None else jnp.maximum(m, cm)
             mbuf[u % SB] = m
 
         def weighted(g, u):
             mc = jnp.max(mbuf[u % SB], axis=0, keepdims=True) * EXP_SCALE
             l = None
             probs = []
-            for start, rows in spans:
-                p = jnp.exp2(y[pl.ds((u % SB) * total + start, rows), :] * EXP_SCALE - mc)
-                ls = jnp.sum(p.reshape(rows // 8, 8, B), axis=0)
-                l = ls if l is None else l + ls
-                probs.append(p.astype(BF16))
+            for start, rows, lane in spans:
+                sc = y[pl.ds((u % SB) * total + start, rows), pl.ds(lane, B - lane)]
+                p = jnp.exp2(sc * EXP_SCALE - mc[:, lane:])
+                ls = jnp.sum(p.reshape(rows // 8, 8, B - lane), axis=0)
+                p = p.astype(BF16)
+                if lane:
+                    l = jnp.concatenate([l[:, :lane], l[:, lane:] + ls], axis=1)
+                    p = jnp.concatenate([jnp.zeros((rows, lane), BF16), p], axis=1)
+                else:
+                    l = ls if l is None else l + ls
+                probs.append(p)
             o = dot(vT[pl.ds(pl.multiple_of(g * HD, HD), HD), pl.ds(0, total)], jnp.concatenate(probs, axis=0))
             return (o * (1.0 / jnp.sum(l, axis=0, keepdims=True))).astype(BF16)
 
-        for u in range(AHEAD):
+        for u in range(ahead_by):
             scores(0, u)
 
         def group_pair(pair, _):
             g = pair * 2
             outs = []
             for u in range(8):
-                ahead = u + AHEAD
+                ahead = u + ahead_by
                 scores(g + ahead // 4 if ahead < 8 else lax.rem(g + 2, KV), ahead)
                 outs.append(weighted(g + u // 4, u))
                 if u % 4 == 3:
@@ -243,37 +263,37 @@
         for n in range(8):
             y[pl.ds(n * B, B), :] = resid[slot, :, pl.ds(n * 256, 256)].astype(F32)
         more = i + 1 < NB
+        wait_gu(0)
+        gate_up(0)
+        start_gu(R, 0, True)
 
         def steps(it, _):
-            again_ok = more | (it < NC // R - 1)
-            c = (it + 1) * R
-            wait_gu(0)
-            wait_gu(1)
-            wait_dn(0)
-            gate_up(0)
-            start_gu(c, 0, again_ok)
-            gate_up(1)
-            start_gu(c + 1, 1, again_ok)
-            down(0)
-            start_dn(c, 0, again_ok)
-            wait_gu(2)
-            wait_dn(1)
-            gate_up(2)
-            start_gu(c + 2, 2, again_ok)
-            down(1)
-            start_dn(c + 1, 1, again_ok)
-            wait_gu(3)
-            wait_dn(2)
-            wait_dn(3)
-            gate_up(3)
-            start_gu(c + 3, 3, again_ok)
-            down(2)
-            start_dn(c + 2, 2, again_ok)
-            down(3)
-            start_dn(c + 3, 3, again_ok)
+            c = it * R
+            for u in range(R):
+                if u % 2 == 0:
+                    wait_gu((u + 1) % R)
+                    wait_gu((u + 2) % R)
+                    wait_dn(u)
+                    wait_dn(u + 1)
+                gate_up((u + 1) % R)
+                start_gu(c + u + 1 + R, (u + 1) % R, more | (c + u + 1 + R < NC))
+                down(u)
+                start_dn(c + u + R, u, more | (c + u + R < NC))
             return 0
 
-        lax.fori_loop(0, NC // R, steps, 0)
+        lax.fori_loop(0, NC // R - 1, steps, 0)
+        for u in range(R):
+            if u % 2 == 0:
+                wait_gu(u + 1)
+                if u + 2 < R:
+                    wait_gu(u + 2)
+                wait_dn(u)
+                wait_dn(u + 1)
+            if u + 1 < R:
+                gate_up(u + 1)
+                start_gu(u + 1, u + 1, more)
+            down(u)
+            start_dn(u, u, more)
         for n in range(8):
             resid[slot, :, pl.ds(n * 256, 256)] = y[pl.ds(n * B, B), :].astype(BF16)
 
@@ -308,15 +328,31 @@
         slot = lax.rem(i, NS)
         emb_copy(i).wait()
 
+        @pl.when(i == 0)
+        def _():
+            for cp in small_copies:
+                cp.wait()
+
         norm(slot, again)
 
         @pl.when(i == 0)
         def _():
-            tab_copy.wait()
             for p in range(6):
                 w_copy(p).wait()
+            for p in range(6, 10):
+                w_copy(p).start()
+            for c in range(2):
+                start_gu(c, c, True)
+                start_dn(c, c, True)
 
         project(i)
+
+        @pl.when(i == 0)
+        def _():
+            for c in range(2, R):
+                start_gu(c, c, True)
+                start_dn(c, c, True)
+
         make_mask(i)
         k_copy(i, 0).start()
         k_copy(i, 1).start()
@@ -393,6 +429,23 @@
 
     for row in range(3):
         piece_copy(row // PER, row % PER)[1].wait()
+
+def place_kernel(hid, k_t, v_t, hid_out, k_out, v_out, hid_v, k_v, v_v, in_sem, out_sem):
+    halves = []
+    for n, (src, buf, dst) in enumerate(((hid, hid_v, hid_out), (k_t, k_v, k_out), (v_t, v_v, v_out))):
+        rows = src.shape[0] // 2
+        for half in range(2):
+            part = pl.ds(half * rows, rows)
+            halves.append((pltpu.make_async_copy(src.at[part], buf.at[part], in_sem.at[n, half]),
+                           pltpu.make_async_copy(buf.at[part], dst.at[part], out_sem.at[n, half])))
+    for load, _ in halves:
+        load.start()
+    for load, store in halves:
+        load.wait()
+        store.start()
+    for _, store in halves:
+        store.wait()
+
 
 def solution(mesh):
     gain_spec = P('stage', None)
@@ -415,11 +468,13 @@
             out_shape=(jax.ShapeDtypeStruct((SEQ // STAGES, D), BF16),
                        jax.ShapeDtypeStruct((KV * HD, SEQ), BF16),
                        jax.ShapeDtypeStruct((KV * HD, SEQ), BF16)),
-            in_specs=[any_spec, smem_spec, vmem_spec, any_spec, any_spec, any_spec, any_spec, vmem_spec,
+            in_specs=[any_spec, smem_spec, any_spec, any_spec, any_spec, any_spec, any_spec, any_spec,
                       any_spec, any_spec, any_spec, any_spec],
             out_specs=(any_spec, any_spec, any_spec),
             scratch_shapes=[
                 pltpu.VMEM((NB, 2, HD // 2, 256), F32),
+                pltpu.VMEM((1, D), F32),
+                pltpu.VMEM((1, D), F32),
                 pltpu.VMEM((3072, D), BF16),
                 pltpu.VMEM((D, D), BF16),
                 [pltpu.VMEM((D, F), BF16)] * R,
@@ -433,9 +488,11 @@
                 pltpu.VMEM((SB * VMAX, B), F32),
                 pltpu.VMEM((SB, 8, B), F32),
                 [pltpu.VMEM((B, F), BF16)] * 2,
-                pltpu.VMEM((B, B), F32),
+                pltpu.VMEM((B // 2, B + B // 2), F32),
                 pltpu.VMEM((VMAX - VMIN, 128), F32),
-                dma((10,)), dma, dma((R,)), dma((R,)), dma((R,)), dma((NS,)), dma((NS,)), dma((3,)), dma((NS, PER)), dma((3,)),
+                pltpu.VMEM((B, 128), BF16),
+                pltpu.VMEM((128, B), BF16),
+                dma((10,)), dma((3,)), dma((R,)), dma((R,)), dma((R,)), dma((NS,)), dma((NS,)), dma((3,)), dma((NS, PER)), dma((3,)),
                 pltpu.SemaphoreType.REGULAR,
             ],
             compiler_params=pltpu.CompilerParams(collective_id=0, has_side_effects=True,
@@ -443,6 +500,16 @@
         )(embeddings, valid_len, attn_gain, wq, wk, wv, wo, mlp_gain, w_gate[0], w_up[0], w_down[0],
           jnp.asarray(table))
 
+        hid, k_t, v_t = pl.pallas_call(
+            place_kernel,
+            name="place",
+            out_shape=tuple(jax.ShapeDtypeStruct(x.shape, BF16) for x in (hid, k_t, v_t)),
+            in_specs=[any_spec] * 3,
+            out_specs=(any_spec,) * 3,
+            scratch_shapes=[pltpu.VMEM(x.shape, BF16) for x in (hid, k_t, v_t)] + [dma((3, 2)), dma((3, 2))],
+            compiler_params=pltpu.CompilerParams(vmem_limit_bytes=67043328),
+        )(hid, k_t, v_t)
+
         def to_cache(x):
             return x.reshape(KV, HD, SEQ).transpose(2, 0, 1)[None]
 

time: 447 us -> 429 us (0.960)
  Pallas kernels: 440 us -> 427 us
  local copies, waits for them, and re-layouts: 5.97 us -> 0 us
    pallas_call x1, Pallas kernels: 440 us -> 423 us  [stage_program(): pl.pallas_call(stage_kernel, name='stage_pipeline', out_shape=(jax.ShapeD...]
    unnamed x7 -> x0, local copies, waits for them, and re-layouts: 5.97 us -> none
where the time goes in v4:
time: 429 us
  Pallas kernels  427 us (100%)
    pallas_call x1, Pallas kernels, stage_program(): pl.pallas_call(stage_kernel, name='stage_pipeline', out_shape=(jax.ShapeD...  423 us

profile of v4, /device:TPU:7, one launch (start us, length us, event | category | flops | bytes accessed | tf_op | source)
XLA Modules:
  0.0 428.7 jit_solution(17687193534599459153)
XLA Ops:
  1.3 423.4 %stage_pipeline.1 = (bf16[384,2048]{1,0:T(8,128)(2,1)}, bf16[512,1536]{1,0:T(8,128)(2,1)}, bf16[512,1536]{1,0:T(8,128)(2,1)}) custom-call(bf16[1536,2048]{1,0:T(8,128)(2,1)} %emb.1, s32[1]{0:T(128)S(6)} %copy.15.valid, f32[1,2048]{1,0:T(1,128)} %again_hbm.1, bf16[2048,2048]{1,0:T(8,128)(2,1)} %bitcast.32, bf16[512,2048]{1,0:T(8,128)(2,1)} %bitcast.34, ...), custom_call_target="tpu_custom_call" | custom-call | tf_op jit(solution)/shard_map/stage_pipeline/pallas_call | solution.py:465
  424.7 4.0 place.1

commit v5 on v4

--- a/solution.py
+++ b/solution.py
@@ -29,6 +29,7 @@
 PIECE = SEQ // STAGES // 3
 PER = B // PIECE
 R = 4
+LENT = R * F
 SB = 4
 EXP_SCALE = math.log2(math.e)
 
@@ -56,11 +57,14 @@
 
 
 def stage_kernel(emb, valid, again_hbm, wq, wk, wv, wo, mgain_hbm, wg, wu, wd, tab_hbm,
-                 hid, kout, vout,
+                 hid, kout, vout, wg_x, wu_x, wd_x,
                  tab, again, mgain, wqkv_v, wo_v, wg_s, wu_s, wd_s, resid, kc, vT, act, qT, y, mbuf, ff_s,
                  mask, vbias, kbias, qones,
-                 w_sem, tab_sem, g_sem, u_sem, d_sem, in_sem, send_sem, kv_sem, piece_sem, out_sem, credit):
+                 w_sem, tab_sem, g_sem, u_sem, d_sem, in_sem, send_sem, kv_sem, piece_sem, out_sem, lend_sem, borrow_sem, pair_sem,
+                 credit):
     stage = lax.axis_index("stage")
+    helper = lax.rem(stage, 2) == 0
+    partner = stage + 1 - 2 * lax.rem(stage, 2)
     barrier = pltpu.get_barrier_semaphore()
     for k in range(1, STAGES):
         pl.semaphore_signal(barrier, inc=1, device_id={"stage": lax.rem(stage + k, STAGES)},
@@ -229,6 +233,31 @@
             o = dot(act[pl.ds(0, B), :], wo_v[:, cols])
             resid[slot, :, cols] = (resid[slot, :, cols].astype(F32) + o).astype(BF16)
 
+    def lend_copies(c):
+        sem = lend_sem
+        cols = pl.ds(pl.multiple_of(FF - LENT + c * F, F), F)
+        rows = pl.ds(pl.multiple_of(c * F, F), F)
+        return [pltpu.make_async_remote_copy(src, dst, sem.at[n], borrow_sem.at[n, c], device_id={"stage": partner},
+                                             device_id_type=pl.DeviceIdType.MESH)
+                for n, (src, dst) in enumerate(((wg.at[:, cols], wg_x.at[:, rows]), (wu.at[:, cols], wu_x.at[:, rows]),
+                                                (wd.at[cols, :], wd_x.at[rows, :])))]
+
+    def borrowed_copies(c):
+        part = pl.ds(c * F, F)
+        return (pltpu.make_async_copy(wg_x.at[:, part], wg_s[c], g_sem.at[c]),
+                pltpu.make_async_copy(wu_x.at[:, part], wu_s[c], u_sem.at[c]),
+                pltpu.make_async_copy(wd_x.at[part, :], wd_s[c], d_sem.at[c]))
+
+    def pair_copy(src, dst, n):
+        return pltpu.make_async_remote_copy(src, dst, pair_sem.at[2 * n], pair_sem.at[2 * n + 1],
+                                            device_id={"stage": partner}, device_id_type=pl.DeviceIdType.MESH)
+
+    def act_copy():
+        return pair_copy(act, act, 0)
+
+    def sum_copy():
+        return pair_copy(y.at[pl.ds(0, 8 * B), :], y.at[pl.ds(8 * B, 8 * B), :], 1)
+
     def gate_up(s):
         x = act[pl.ds(0, B), :]
         gate = dot(x, wg_s[s][...])
@@ -259,13 +288,13 @@
         def _():
             dn_copy(lax.rem(c, NC), s).start()
 
-    def mlp(i, slot):
-        for n in range(8):
-            y[pl.ds(n * B, B), :] = resid[slot, :, pl.ds(n * 256, 256)].astype(F32)
+    def mlp(i):
         more = i + 1 < NB
+        shared = (i == NB - 1) & jnp.logical_not(helper)
+        mine = jnp.where(shared, NC - R, NC)
         wait_gu(0)
         gate_up(0)
-        start_gu(R, 0, True)
+        start_gu(R, 0, i < NB)
 
         def steps(it, _):
             c = it * R
@@ -276,12 +305,12 @@
                     wait_dn(u)
                     wait_dn(u + 1)
                 gate_up((u + 1) % R)
-                start_gu(c + u + 1 + R, (u + 1) % R, more | (c + u + 1 + R < NC))
+                start_gu(c + u + 1 + R, (u + 1) % R, more | (c + u + 1 + R < mine))
                 down(u)
-                start_dn(c + u + R, u, more | (c + u + R < NC))
+                start_dn(c + u + R, u, more | (c + u + R < mine))
             return 0
 
-        lax.fori_loop(0, NC // R - 1, steps, 0)
+        lax.fori_loop(0, jnp.where(i < NB, jnp.where(shared, NC // R - 2, NC // R - 1), 0), steps, 0)
         for u in range(R):
             if u % 2 == 0:
                 wait_gu(u + 1)
@@ -294,8 +323,6 @@
                 start_gu(u + 1, u + 1, more)
             down(u)
             start_dn(u, u, more)
-        for n in range(8):
-            resid[slot, :, pl.ds(n * 256, 256)] = y[pl.ds(n * B, B), :].astype(BF16)
 
     def next_copy(i):
         slot = lax.rem(i, NS)
@@ -326,102 +353,150 @@
 
     def block(i, _):
         slot = lax.rem(i, NS)
-        emb_copy(i).wait()
-
-        @pl.when(i == 0)
-        def _():
-            for cp in small_copies:
-                cp.wait()
-
-        norm(slot, again)
-
-        @pl.when(i == 0)
-        def _():
-            for p in range(6):
-                w_copy(p).wait()
-            for p in range(6, 10):
-                w_copy(p).start()
-            for c in range(2):
-                start_gu(c, c, True)
-                start_dn(c, c, True)
-
-        project(i)
-
-        @pl.when(i == 0)
-        def _():
-            for c in range(2, R):
-                start_gu(c, c, True)
-                start_dn(c, c, True)
-
-        make_mask(i)
-        k_copy(i, 0).start()
-        k_copy(i, 1).start()
-        v_copy(i).start()
+        main = i < NB
+        shared = (i == NB - 1) & jnp.logical_not(helper)
+
+        @pl.when(main)
+        def _():
+            emb_copy(i).wait()
+
+            @pl.when(i == 0)
+            def _():
+                for cp in small_copies:
+                    cp.wait()
+
+            norm(slot, again)
+
+            @pl.when(i == 0)
+            def _():
+                for p in range(6):
+                    w_copy(p).wait()
+                for p in range(6, 10):
+                    w_copy(p).start()
+                for c in range(2):
+                    start_gu(c, c, True)
+                    start_dn(c, c, True)
+
+            project(i)
+
+            @pl.when(i == 0)
+            def _():
+                for c in range(2, R):
+                    start_gu(c, c, True)
+                    start_dn(c, c, True)
+                pl.semaphore_wait(barrier, STAGES - 1)
+
+            make_mask(i)
+            k_copy(i, 0).start()
+            k_copy(i, 1).start()
+            v_copy(i).start()
+
+            @pl.when(jnp.logical_not(helper) & (i < R))
+            def _():
+                for cp in lend_copies(i):
+                    cp.start()
+
         for n in range(NB):
             @pl.when(i == n)
             def _():
                 attend(n)
 
-        @pl.when(i == 0)
-        def _():
-            pl.semaphore_wait(barrier, STAGES - 1)
-
-        @pl.when((i >= 1) & jnp.logical_not(last))
-        def _():
-            next_copy(i - 1).wait_send()
-
-        for r in range(PER):
-            remote, local, mine = piece_copy(i - 1, r)
-
-            @pl.when((i >= 1) & last & jnp.logical_not(mine))
-            def _():
-                remote.wait_send()
-
-        @pl.when((stage > 0) & (i >= 1) & (i - 1 + NS < NB))
-        def _():
-            pl.semaphore_signal(credit, inc=1, device_id={"stage": lax.rem(stage + STAGES - 1, STAGES)},
-                                device_id_type=pl.DeviceIdType.MESH)
-
-        @pl.when((stage == 0) & (i + 1 < NB))
-        def _():
-            emb_copy(i + 1).start()
-
-
-        @pl.when(i == 0)
-        def _():
-            for p in range(6, 10):
-                w_copy(p).wait()
-
-        k_copy(i, 0).wait()
-        k_copy(i, 1).wait()
-        v_copy(i).wait()
-        out_proj(slot)
-        norm(slot, mgain)
-        mlp(i, slot)
-
-
-        @pl.when(jnp.logical_not(last) & (i >= NS))
-        def _():
-            pl.semaphore_wait(credit, 1)
-
-        @pl.when(jnp.logical_not(last))
-        def _():
-            next_copy(i).start()
-
-        for r in range(PER):
-            remote, local, mine = piece_copy(i, r)
-
-            @pl.when(last & jnp.logical_not(mine))
-            def _():
-                remote.start()
-
-            @pl.when(last & mine)
-            def _():
-                local.start()
+        @pl.when(main)
+        def _():
+            @pl.when((i >= 1) & jnp.logical_not(last))
+            def _():
+                next_copy(i - 1).wait_send()
+
+            for r in range(PER):
+                remote, local, mine = piece_copy(i - 1, r)
+
+                @pl.when((i >= 1) & last & jnp.logical_not(mine))
+                def _():
+                    remote.wait_send()
+
+            @pl.when((stage > 0) & (i >= 1) & (i - 1 + NS < NB))
+            def _():
+                pl.semaphore_signal(credit, inc=1, device_id={"stage": lax.rem(stage + STAGES - 1, STAGES)},
+                                    device_id_type=pl.DeviceIdType.MESH)
+
+            @pl.when((stage == 0) & (i + 1 < NB))
+            def _():
+                emb_copy(i + 1).start()
+
+            @pl.when(i == 0)
+            def _():
+                for p in range(6, 10):
+                    w_copy(p).wait()
+
+            @pl.when(jnp.logical_not(helper) & (i < R))
+            def _():
+                for cp in lend_copies(i):
+                    cp.wait_send()
+
+            k_copy(i, 0).wait()
+            k_copy(i, 1).wait()
+            v_copy(i).wait()
+            out_proj(slot)
+            norm(slot, mgain)
+            for n in range(8):
+                y[pl.ds(n * B, B), :] = resid[slot, :, pl.ds(n * 256, 256)].astype(F32)
+
+            @pl.when(shared)
+            def _():
+                act_copy().start()
+
+        @pl.when(jnp.logical_not(main))
+        def _():
+            for c in range(R):
+                for cp in lend_copies(c):
+                    cp.wait_recv()
+                for cp in borrowed_copies(c):
+                    cp.start()
+            y[pl.ds(0, 8 * B), :] = jnp.zeros((8 * B, B), F32)
+            act_copy().wait_recv()
+
+        mlp(i)
+
+        @pl.when(shared)
+        def _():
+            act_copy().wait_send()
+            sum_copy().wait_recv()
+            for n in range(8):
+                rows = pl.ds(n * B, B)
+                y[rows, :] = y[rows, :] + y[pl.ds((n + 8) * B, B), :]
+
+        @pl.when(jnp.logical_not(main))
+        def _():
+            sum_copy().start()
+            sum_copy().wait_send()
+
+        @pl.when(main)
+        def _():
+            for n in range(8):
+                resid[slot, :, pl.ds(n * 256, 256)] = y[pl.ds(n * B, B), :].astype(BF16)
+
+            @pl.when(jnp.logical_not(last) & (i >= NS))
+            def _():
+                pl.semaphore_wait(credit, 1)
+
+            @pl.when(jnp.logical_not(last))
+            def _():
+                next_copy(i).start()
+
+            for r in range(PER):
+                remote, local, mine = piece_copy(i, r)
+
+                @pl.when(last & jnp.logical_not(mine))
+                def _():
+                    remote.start()
+
+                @pl.when(last & mine)
+                def _():
+                    local.start()
 
         return 0
 
-    lax.fori_loop(0, NB, block, 0)
+    lax.fori_loop(0, NB + jnp.where(helper, 1, 0), block, 0)
 
     @pl.when(jnp.logical_not(last))
     def _():
@@ -462,15 +537,18 @@
         any_spec = pl.BlockSpec(memory_space=pl.ANY)
         vmem_spec = pl.BlockSpec(memory_space=pltpu.VMEM)
         smem_spec = pl.BlockSpec(memory_space=pltpu.SMEM)
-        hid, k_t, v_t = pl.pallas_call(
+        hid, k_t, v_t, _, _, _ = pl.pallas_call(
             stage_kernel,
             name="stage_pipeline",
             out_shape=(jax.ShapeDtypeStruct((SEQ // STAGES, D), BF16),
                        jax.ShapeDtypeStruct((KV * HD, SEQ), BF16),
-                       jax.ShapeDtypeStruct((KV * HD, SEQ), BF16)),
+                       jax.ShapeDtypeStruct((KV * HD, SEQ), BF16),
+                       jax.ShapeDtypeStruct((D, LENT), BF16),
+                       jax.ShapeDtypeStruct((D, LENT), BF16),
+                       jax.ShapeDtypeStruct((LENT, D), BF16)),
             in_specs=[any_spec, smem_spec, any_spec, any_spec, any_spec, any_spec, any_spec, any_spec,
                       any_spec, any_spec, any_spec, any_spec],
-            out_specs=(any_spec, any_spec, any_spec),
+            out_specs=(any_spec,) * 6,
             scratch_shapes=[
                 pltpu.VMEM((NB, 2, HD // 2, 256), F32),
                 pltpu.VMEM((1, D), F32),
@@ -493,6 +571,7 @@
                 pltpu.VMEM((B, 128), BF16),
                 pltpu.VMEM((128, B), BF16),
                 dma((10,)), dma((3,)), dma((R,)), dma((R,)), dma((R,)), dma((NS,)), dma((NS,)), dma((3,)), dma((NS, PER)), dma((3,)),
+                dma((3,)), dma((3, R)), dma((4,)),
                 pltpu.SemaphoreType.REGULAR,
             ],
             compiler_params=pltpu.CompilerParams(collective_id=0, has_side_effects=True,

time: 429 us -> 425 us (level)
  no operation moved by 1% of the time
where the time goes in v5:
time: 425 us
  Pallas kernels  424 us (100%)
    pallas_call x1, Pallas kernels, stage_program(): pl.pallas_call(stage_kernel, name='stage_pipeline', out_shape=(jax.ShapeD...  420 us

profile of v5, /device:TPU:7, one launch (start us, length us, event | category | flops | bytes accessed | tf_op | source)
XLA Modules:
  0.0 424.9 jit_solution(10705716417430690843)
XLA Ops:
  1.3 419.7 %stage_pipeline.1 = (bf16[384,2048]{1,0:T(8,128)(2,1)}, bf16[512,1536]{1,0:T(8,128)(2,1)}, bf16[512,1536]{1,0:T(8,128)(2,1)}, bf16[2048,2048]{1,0:T(8,128)(2,1)}...) custom-call(bf16[1536,2048]{1,0:T(8,128)(2,1)} %emb.1, s32[1]{0:T(128)S(6)} %copy.15.valid, f32[1,2048]{1,0:T(1,128)} %again_hbm.1, ...), custom_call_target="tpu_custom_call" | custom-call | tf_op jit(solution)/shard_map/stage_pipeline/pallas_call | solution.py:540
  421.0 4.0 place.1

commit v6 on v5

--- a/solution.py
+++ b/solution.py
@@ -117,11 +117,18 @@
     row = lax.broadcasted_iota(jnp.int32, qones.shape, 0)
     qones[...] = jnp.where(row == 0, 1.0, 0.0).astype(BF16)
 
-    def norm(slot, gain_ref):
+    def norm(slot, gain_ref, main=None):
         for r in range(0, B, 16):
             x = resid[slot, pl.ds(r, 16), :].astype(F32)
             inv = lax.rsqrt(jnp.mean(x * x, axis=-1, keepdims=True) + EPS)
-            act[pl.ds(r, 16), :] = (x * inv * gain_ref[...]).astype(BF16)
+            x = (x * inv * gain_ref[...]).astype(BF16)
+            for half in range(2):
+                cols = slice(half * (D // 2), (half + 1) * (D // 2))
+                part = x[:, cols]
+                if main is not None:
+                    sent = qT[half * 2 + r // 128, pl.ds(r % 128, 16), :]
+                    part = jnp.where(main, part.astype(F32), sent.astype(F32)).astype(BF16)
+                act[pl.ds(r, 16), cols] = part
 
     def rope(x, cos, sin):
         front = x[:HD // 2]
@@ -140,9 +147,6 @@
             kh = jnp.concatenate(parts[half * 8:half * 8 + 8], axis=0).astype(BF16)
             ff_s[1][:, pl.ds(half * 256, 256)] = kh
             kc[pl.ds(pl.multiple_of(i * B, B), B), pl.ds(half * 256, 256)] = kh.T
-        vt = dot_t(wqkv_v[pl.ds(2560, 512), :], act[...])
-        vT[:, pl.ds(pl.multiple_of(i * B, B), B)] = vt.astype(BF16)
-
         for pair in range(4):
             qt = dot_t(wqkv_v[pl.ds(pair * 512, 512), :], act[...])
             for h in range(8):
@@ -152,6 +156,9 @@
                 cols = pl.ds((h % 4) * B, B)
                 qT[g, pl.ds(row, HD // 2), cols] = (f * 0.125).astype(BF16)
                 qT[g, pl.ds(row + HD // 2, HD // 2), cols] = (b * 0.125).astype(BF16)
+
+        vt = dot_t(wqkv_v[pl.ds(2560, 512), :], act[...])
+        vT[:, pl.ds(pl.multiple_of(i * B, B), B)] = vt.astype(BF16)
 
     def make_mask(i):
         key = lax.broadcasted_iota(jnp.int32, mask.shape, 0)
@@ -210,6 +217,9 @@
             o = dot(vT[pl.ds(pl.multiple_of(g * HD, HD), HD), pl.ds(0, total)], jnp.concatenate(probs, axis=0))
             return (o * (1.0 / jnp.sum(l, axis=0, keepdims=True))).astype(BF16)
 
+        def put_out(g):
+            act[:, pl.ds(pl.multiple_of(g * 256, 256), 256)] = ff_s[0][:, pl.ds(0, 256)].T
+
         for u in range(ahead_by):
             scores(0, u)
 
@@ -220,12 +230,17 @@
                 ahead = u + ahead_by
                 scores(g + ahead // 4 if ahead < 8 else lax.rem(g + 2, KV), ahead)
                 outs.append(weighted(g + u // 4, u))
-                if u % 4 == 3:
-                    act[:, pl.ds(pl.multiple_of((g + u // 4) * 256, 256), 256)] = jnp.concatenate(outs, axis=0).T
+                if u == 0:
+                    put_out(lax.rem(g + KV - 1, KV))
+                if u == 3:
+                    act[:, pl.ds(pl.multiple_of(g * 256, 256), 256)] = jnp.concatenate(outs, axis=0).T
                     outs = []
+            for h in range(4):
+                ff_s[0][pl.ds(h * HD, HD), pl.ds(0, 256)] = outs[h]
             return 0
 
         lax.fori_loop(0, KV // 2, group_pair, 0)
+        put_out(KV - 1)
 
     def out_proj(slot):
         for n in range(4):
@@ -249,14 +264,15 @@
                 pltpu.make_async_copy(wd_x.at[part, :], wd_s[c], d_sem.at[c]))
 
     def pair_copy(src, dst, n):
-        return pltpu.make_async_remote_copy(src, dst, pair_sem.at[2 * n], pair_sem.at[2 * n + 1],
+        return pltpu.make_async_remote_copy(src, dst, pair_sem.at[0, n], pair_sem.at[1, n],
                                             device_id={"stage": partner}, device_id_type=pl.DeviceIdType.MESH)
 
-    def act_copy():
-        return pair_copy(act, act, 0)
+    def act_copies():
+        return [pair_copy(act.at[pl.ds(r * 128, 128), pl.ds(half * 1024, 1024)], qT.at[half * 2 + r], half * 2 + r)
+                for half in range(2) for r in range(2)]
 
     def sum_copy():
-        return pair_copy(y.at[pl.ds(0, 8 * B), :], y.at[pl.ds(8 * B, 8 * B), :], 1)
+        return pair_copy(y.at[pl.ds(0, 8 * B), :], y.at[pl.ds(8 * B, 8 * B), :], 4)
 
     def gate_up(s):
         x = act[pl.ds(0, B), :]
@@ -436,14 +452,6 @@
             k_copy(i, 0).wait()
             k_copy(i, 1).wait()
             v_copy(i).wait()
-            out_proj(slot)
-            norm(slot, mgain)
-            for n in range(8):
-                y[pl.ds(n * B, B), :] = resid[slot, :, pl.ds(n * 256, 256)].astype(F32)
-
-            @pl.when(shared)
-            def _():
-                act_copy().start()
 
         @pl.when(jnp.logical_not(main))
         def _():
@@ -452,18 +460,32 @@
                     cp.wait_recv()
                 for cp in borrowed_copies(c):
                     cp.start()
-            y[pl.ds(0, 8 * B), :] = jnp.zeros((8 * B, B), F32)
-            act_copy().wait_recv()
+            for cp in act_copies():
+                cp.wait_recv()
+
+        out_proj(slot)
+        norm(slot, mgain, main)
+        for n in range(8):
+            h = resid[slot, :, pl.ds(n * 256, 256)].astype(F32)
+            y[pl.ds(n * B, B), :] = jnp.where(main, h, 0.0)
+
+        @pl.when(shared)
+        def _():
+            for cp in act_copies():
+                cp.start()
 
         mlp(i)
+        for n in range(8):
+            resid[slot, :, pl.ds(n * 256, 256)] = y[pl.ds(n * B, B), :].astype(BF16)
 
         @pl.when(shared)
         def _():
-            act_copy().wait_send()
+            for cp in act_copies():
+                cp.wait_send()
             sum_copy().wait_recv()
             for n in range(8):
-                rows = pl.ds(n * B, B)
-                y[rows, :] = y[rows, :] + y[pl.ds((n + 8) * B, B), :]
+                h = y[pl.ds(n * B, B), :] + y[pl.ds((n + 8) * B, B), :]
+                resid[slot, :, pl.ds(n * 256, 256)] = h.astype(BF16)
 
         @pl.when(jnp.logical_not(main))
         def _():
@@ -472,9 +494,6 @@
 
         @pl.when(main)
         def _():
-            for n in range(8):
-                resid[slot, :, pl.ds(n * 256, 256)] = y[pl.ds(n * B, B), :].astype(BF16)
-
             @pl.when(jnp.logical_not(last) & (i >= NS))
             def _():
                 pl.semaphore_wait(credit, 1)
@@ -571,7 +590,7 @@
                 pltpu.VMEM((B, 128), BF16),
                 pltpu.VMEM((128, B), BF16),
                 dma((10,)), dma((3,)), dma((R,)), dma((R,)), dma((R,)), dma((NS,)), dma((NS,)), dma((3,)), dma((NS, PER)), dma((3,)),
-                dma((3,)), dma((3, R)), dma((4,)),
+                dma((3,)), dma((3, R)), dma((2, 5)),
                 pltpu.SemaphoreType.REGULAR,
             ],
             compiler_params=pltpu.CompilerParams(collective_id=0, has_side_effects=True,

time: 425 us -> 427 us (level)
  no operation moved by 1% of the time
where the time goes in v6:
time: 427 us
  Pallas kernels  425 us (100%)
    pallas_call x1, Pallas kernels, stage_program(): pl.pallas_call(stage_kernel, name='stage_pipeline', out_shape=(jax.ShapeD...  421 us

profile of v6, /device:TPU:7, one launch (start us, length us, event | category | flops | bytes accessed | tf_op | source)
XLA Modules:
  0.0 426.6 jit_solution(7627609044915248289)
XLA Ops:
  1.3 421.3 %stage_pipeline.1 = (bf16[384,2048]{1,0:T(8,128)(2,1)}, bf16[512,1536]{1,0:T(8,128)(2,1)}, bf16[512,1536]{1,0:T(8,128)(2,1)}, bf16[2048,2048]{1,0:T(8,128)(2,1)}...) custom-call(bf16[1536,2048]{1,0:T(8,128)(2,1)} %emb.1, s32[1]{0:T(128)S(6)} %copy.15.valid, f32[1,2048]{1,0:T(1,128)} %again_hbm.1, ...), custom_call_target="tpu_custom_call" | custom-call | tf_op jit(solution)/shard_map/stage_pipeline/pallas_call | solution.py:559
  422.6 4.0 place.1

commit v7 on v5

--- a/solution.py
+++ b/solution.py
@@ -210,6 +210,9 @@
             o = dot(vT[pl.ds(pl.multiple_of(g * HD, HD), HD), pl.ds(0, total)], jnp.concatenate(probs, axis=0))
             return (o * (1.0 / jnp.sum(l, axis=0, keepdims=True))).astype(BF16)
 
+        def put_out(g):
+            act[:, pl.ds(pl.multiple_of(g * 256, 256), 256)] = ff_s[0][:, pl.ds(0, 256)].T
+
         for u in range(ahead_by):
             scores(0, u)
 
@@ -220,12 +223,17 @@
                 ahead = u + ahead_by
                 scores(g + ahead // 4 if ahead < 8 else lax.rem(g + 2, KV), ahead)
                 outs.append(weighted(g + u // 4, u))
-                if u % 4 == 3:
-                    act[:, pl.ds(pl.multiple_of((g + u // 4) * 256, 256), 256)] = jnp.concatenate(outs, axis=0).T
+                if u == 0:
+                    put_out(lax.rem(g + KV - 1, KV))
+                if u == 3:
+                    act[:, pl.ds(pl.multiple_of(g * 256, 256), 256)] = jnp.concatenate(outs, axis=0).T
                     outs = []
+            for h in range(4):
+                ff_s[0][pl.ds(h * HD, HD), pl.ds(0, 256)] = outs[h]
             return 0
 
         lax.fori_loop(0, KV // 2, group_pair, 0)
+        put_out(KV - 1)
 
     def out_proj(slot):
         for n in range(4):
@@ -391,11 +399,6 @@
             k_copy(i, 1).start()
             v_copy(i).start()
 
-            @pl.when(jnp.logical_not(helper) & (i < R))
-            def _():
-                for cp in lend_copies(i):
-                    cp.start()
-
         for n in range(NB):
             @pl.when(i == n)
             def _():
@@ -427,11 +430,6 @@
             def _():
                 for p in range(6, 10):
                     w_copy(p).wait()
-
-            @pl.when(jnp.logical_not(helper) & (i < R))
-            def _():
-                for cp in lend_copies(i):
-                    cp.wait_send()
 
             k_copy(i, 0).wait()
             k_copy(i, 1).wait()
@@ -456,14 +454,16 @@
             act_copy().wait_recv()
 
         mlp(i)
+        for n in range(8):
+            resid[slot, :, pl.ds(n * 256, 256)] = y[pl.ds(n * B, B), :].astype(BF16)
 
         @pl.when(shared)
         def _():
             act_copy().wait_send()
             sum_copy().wait_recv()
             for n in range(8):
-                rows = pl.ds(n * B, B)
-                y[rows, :] = y[rows, :] + y[pl.ds((n + 8) * B, B), :]
+                h = y[pl.ds(n * B, B), :] + y[pl.ds((n + 8) * B, B), :]
+                resid[slot, :, pl.ds(n * 256, 256)] = h.astype(BF16)
 
         @pl.when(jnp.logical_not(main))
         def _():
@@ -472,9 +472,6 @@
 
         @pl.when(main)
         def _():
-            for n in range(8):
-                resid[slot, :, pl.ds(n * 256, 256)] = y[pl.ds(n * B, B), :].astype(BF16)
-
             @pl.when(jnp.logical_not(last) & (i >= NS))
             def _():
                 pl.semaphore_wait(credit, 1)
@@ -493,6 +490,16 @@
                 @pl.when(last & mine)
                 def _():
                     local.start()
+
+            @pl.when(jnp.logical_not(helper) & (i >= 1) & (i <= R))
+            def _():
+                for cp in lend_copies(i - 1):
+                    cp.wait_send()
+
+            @pl.when(jnp.logical_not(helper) & (i < R))
+            def _():
+                for cp in lend_copies(i):
+                    cp.start()
 
         return 0
 

time: 425 us -> 418 us (0.984)
  Pallas kernels: 424 us -> 416 us
    pallas_call x1, Pallas kernels: 420 us -> 412 us  [stage_program(): pl.pallas_call(stage_kernel, name='stage_pipeline', out_shape=(jax.ShapeD...]
where the time goes in v7:
time: 418 us
  Pallas kernels  416 us (100%)
    pallas_call x1, Pallas kernels, stage_program(): pl.pallas_call(stage_kernel, name='stage_pipeline', out_shape=(jax.ShapeD...  412 us

profile of v7, /device:TPU:7, one launch (start us, length us, event | category | flops | bytes accessed | tf_op | source)
XLA Modules:
  0.0 417.7 jit_solution(17166945218590579946)
XLA Ops:
  1.3 412.4 %stage_pipeline.1 = (bf16[384,2048]{1,0:T(8,128)(2,1)}, bf16[512,1536]{1,0:T(8,128)(2,1)}, bf16[512,1536]{1,0:T(8,128)(2,1)}, bf16[2048,2048]{1,0:T(8,128)(2,1)}...) custom-call(bf16[1536,2048]{1,0:T(8,128)(2,1)} %emb.1, s32[1]{0:T(128)S(6)} %copy.15.valid, f32[1,2048]{1,0:T(1,128)} %again_hbm.1, ...), custom_call_target="tpu_custom_call" | custom-call | tf_op jit(solution)/shard_map/stage_pipeline/pallas_call | solution.py:547
  413.7 4.0 place.1

commit v8 on v7

--- a/solution.py
+++ b/solution.py
@@ -29,6 +29,7 @@
 PIECE = SEQ // STAGES // 3
 PER = B // PIECE
 R = 4
+LEND_AT = (NC - R + (NC - R) * (NB - 1)) % NC * F
 LENT = R * F
 SB = 4
 EXP_SCALE = math.log2(math.e)
@@ -243,7 +244,7 @@
 
     def lend_copies(c):
         sem = lend_sem
-        cols = pl.ds(pl.multiple_of(FF - LENT + c * F, F), F)
+        cols = pl.ds(pl.multiple_of(LEND_AT + c * F, F), F)
         rows = pl.ds(pl.multiple_of(c * F, F), F)
         return [pltpu.make_async_remote_copy(src, dst, sem.at[n], borrow_sem.at[n, c], device_id={"stage": partner},
                                              device_id_type=pl.DeviceIdType.MESH)
@@ -266,17 +267,17 @@
     def sum_copy():
         return pair_copy(y.at[pl.ds(0, 8 * B), :], y.at[pl.ds(8 * B, 8 * B), :], 1)
 
-    def gate_up(s):
-        x = act[pl.ds(0, B), :]
+    def gate_up(s, first=0, rows=B):
+        x = act[pl.ds(first, rows), :]
         gate = dot(x, wg_s[s][...])
         up = dot(x, wu_s[s][...])
-        ff_s[s % 2][...] = (gate * jax.nn.sigmoid(gate) * up).astype(BF16)
-
-    def down(s):
-        x = ff_s[s % 2][...]
+        ff_s[s % 2][pl.ds(first, rows), :] = (gate * jax.nn.sigmoid(gate) * up).astype(BF16)
+
+    def down(s, first=0, rows=B):
+        x = ff_s[s % 2][pl.ds(first, rows), :]
         for n in range(8):
-            rows = pl.ds(n * B, B)
-            y[rows, :] = y[rows, :] + dot(x, wd_s[s][:, pl.ds(n * 256, 256)])
+            part = pl.ds(n * B + first, rows)
+            y[part, :] = y[part, :] + dot(x, wd_s[s][:, pl.ds(n * 256, 256)])
 
     def wait_gu(s):
         for cp in gu_copy(0, s):
@@ -296,45 +297,58 @@
         def _():
             dn_copy(lax.rem(c, NC), s).start()
 
-    def mlp(i):
-        more = i + 1 < NB
+    def mlp(i, half_done):
         shared = (i == NB - 1) & jnp.logical_not(helper)
         mine = jnp.where(shared, NC - R, NC)
-        wait_gu(0)
+
+        def fetch(start, idx, slot):
+            start(idx + (NC - R) * i, slot, (i < NB) & (idx < mine))
+
+        @pl.when((i == 0) | (i == NB))
+        def _():
+            wait_gu(0)
+
         gate_up(0)
-        start_gu(R, 0, i < NB)
+        fetch(start_gu, R, 0)
 
         def steps(it, _):
             c = it * R
             for u in range(R):
                 if u % 2 == 0:
-                    wait_gu((u + 1) % R)
-                    wait_gu((u + 2) % R)
+                    @pl.when((i == 0) | (it > 0))
+                    def _():
+                        wait_gu(u + 1)
+                        wait_dn(u)
+                        wait_dn(u + 1)
+                        if u + 2 < R:
+                            wait_gu(u + 2)
+
+                    if u + 2 == R:
+                        wait_gu(0)
+                gate_up((u + 1) % R)
+                fetch(start_gu, c + u + 1 + R, (u + 1) % R)
+                down(u)
+                fetch(start_dn, c + u + R, u)
+            return 0
+
+        lax.fori_loop(0, jnp.where(i < NB, jnp.where(shared, NC // R - 2, NC // R - 1), 0), steps, 0)
+        for half in range(2):
+            for u in range(R):
+                if u % 2 == 0 and half == 0:
+                    wait_gu(u + 1)
+                    if u + 2 < R:
+                        wait_gu(u + 2)
                     wait_dn(u)
                     wait_dn(u + 1)
-                gate_up((u + 1) % R)
-                start_gu(c + u + 1 + R, (u + 1) % R, more | (c + u + 1 + R < mine))
-                down(u)
-                start_dn(c + u + R, u, more | (c + u + R < mine))
-            return 0
-
-        lax.fori_loop(0, jnp.where(i < NB, jnp.where(shared, NC // R - 2, NC // R - 1), 0), steps, 0)
-        for u in range(R):
-            if u % 2 == 0:
-                wait_gu(u + 1)
-                if u + 2 < R:
-                    wait_gu(u + 2)
-                wait_dn(u)
-                wait_dn(u + 1)
-            if u + 1 < R:
-                gate_up(u + 1)
-                start_gu(u + 1, u + 1, more)
-            down(u)
-            start_dn(u, u, more)
-
-    def next_copy(i):
+                if u + 1 < R:
+                    gate_up(u + 1, half * PIECE, PIECE)
+                down(u, half * PIECE, PIECE)
+            half_done(half)
+
+    def next_copy(i, r):
         slot = lax.rem(i, NS)
-        return pltpu.make_async_remote_copy(resid.at[slot], resid.at[slot], send_sem.at[slot], in_sem.at[slot],
+        part = resid.at[slot, pl.ds(r * PIECE, PIECE), :]
+        return pltpu.make_async_remote_copy(part, part, send_sem.at[slot, r], in_sem.at[slot],
                                             device_id={"stage": lax.rem(stage + 1, STAGES)},
                                             device_id_type=pl.DeviceIdType.MESH)
 
@@ -408,7 +422,8 @@
         def _():
             @pl.when((i >= 1) & jnp.logical_not(last))
             def _():
-                next_copy(i - 1).wait_send()
+                for r in range(PER):
+                    next_copy(i - 1, r).wait_send()
 
             for r in range(PER):
                 remote, local, mine = piece_copy(i - 1, r)
@@ -430,6 +445,10 @@
             def _():
                 for p in range(6, 10):
                     w_copy(p).wait()
+
+            @pl.when(jnp.logical_not(last) & (i >= NS))
+            def _():
+                pl.semaphore_wait(credit, 1)
 
             k_copy(i, 0).wait()
             k_copy(i, 1).wait()
@@ -453,9 +472,28 @@
             y[pl.ds(0, 8 * B), :] = jnp.zeros((8 * B, B), F32)
             act_copy().wait_recv()
 
-        mlp(i)
-        for n in range(8):
-            resid[slot, :, pl.ds(n * 256, 256)] = y[pl.ds(n * B, B), :].astype(BF16)
+        def send(r, ok):
+            remote, local, mine = piece_copy(i, r)
+
+            @pl.when(ok & jnp.logical_not(last))
+            def _():
+                next_copy(i, r).start()
+
+            @pl.when(ok & last & jnp.logical_not(mine))
+            def _():
+                remote.start()
+
+            @pl.when(ok & last & mine)
+            def _():
+                local.start()
+
+        def half_done(half):
+            for n in range(8):
+                resid[slot, pl.ds(half * PIECE, PIECE), pl.ds(n * 256, 256)] = \
+                    y[pl.ds(n * B + half * PIECE, PIECE), :].astype(BF16)
+            send(half, main & jnp.logical_not(shared))
+
+        mlp(i, half_done)
 
         @pl.when(shared)
         def _():
@@ -465,6 +503,9 @@
                 h = y[pl.ds(n * B, B), :] + y[pl.ds((n + 8) * B, B), :]
                 resid[slot, :, pl.ds(n * 256, 256)] = h.astype(BF16)
 
+        for r in range(PER):
+            send(r, shared)
+
         @pl.when(jnp.logical_not(main))
         def _():
             sum_copy().start()
@@ -472,25 +513,6 @@
 
         @pl.when(main)
         def _():
-            @pl.when(jnp.logical_not(last) & (i >= NS))
-            def _():
-                pl.semaphore_wait(credit, 1)
-
-            @pl.when(jnp.logical_not(last))
-            def _():
-                next_copy(i).start()
-
-            for r in range(PER):
-                remote, local, mine = piece_copy(i, r)
-
-                @pl.when(last & jnp.logical_not(mine))
-                def _():
-                    remote.start()
-
-                @pl.when(last & mine)
-                def _():
-                    local.start()
-
             @pl.when(jnp.logical_not(helper) & (i >= 1) & (i <= R))
             def _():
                 for cp in lend_copies(i - 1):
@@ -507,7 +529,8 @@
 
     @pl.when(jnp.logical_not(last))
     def _():
-        next_copy(NB - 1).wait_send()
+        for r in range(PER):
+            next_copy(NB - 1, r).wait_send()
 
     for row in range(3):
         piece_copy(row // PER, row % PER)[1].wait()
@@ -577,7 +600,7 @@
                 pltpu.VMEM((VMAX - VMIN, 128), F32),
                 pltpu.VMEM((B, 128), BF16),
                 pltpu.VMEM((128, B), BF16),
-                dma((10,)), dma((3,)), dma((R,)), dma((R,)), dma((R,)), dma((NS,)), dma((NS,)), dma((3,)), dma((NS, PER)), dma((3,)),
+                dma((10,)), dma((3,)), dma((R,)), dma((R,)), dma((R,)), dma((NS,)), dma((NS, PER)), dma((3,)), dma((NS, PER)), dma((3,)),
                 dma((3,)), dma((3, R)), dma((4,)),
                 pltpu.SemaphoreType.REGULAR,
             ],

time: 418 us -> 416 us (level)
  no operation moved by 1% of the time
where the time goes in v8:
time: 416 us
  Pallas kernels  414 us (100%)
    pallas_call x1, Pallas kernels, stage_program(): pl.pallas_call(stage_kernel, name='stage_pipeline', out_shape=(jax.ShapeD...  410 us

profile of v8, /device:TPU:7, one launch (start us, length us, event | category | flops | bytes accessed | tf_op | source)
XLA Modules:
  0.0 415.5 jit_solution(12064914501699900707)
XLA Ops:
  1.3 410.3 %stage_pipeline.1 = (bf16[384,2048]{1,0:T(8,128)(2,1)}, bf16[512,1536]{1,0:T(8,128)(2,1)}, bf16[512,1536]{1,0:T(8,128)(2,1)}, bf16[2048,2048]{1,0:T(8,128)(2,1)}...) custom-call(bf16[1536,2048]{1,0:T(8,128)(2,1)} %emb.1, s32[1]{0:T(128)S(6)} %copy.15.valid, f32[1,2048]{1,0:T(1,128)} %again_hbm.1, ...), custom_call_target="tpu_custom_call" | custom-call | tf_op jit(solution)/shard_map/stage_pipeline/pallas_call | solution.py:570
  411.5 4.0 place.1

commit v9 on v8

--- a/solution.py
+++ b/solution.py
@@ -382,6 +382,10 @@
         def _():
             emb_copy(i).wait()
 
+            @pl.when((stage == 0) & (i >= 1) & (i + 1 < NB))
+            def _():
+                emb_copy(i + 1).start()
+
             @pl.when(i == 0)
             def _():
                 for cp in small_copies:
@@ -437,9 +441,9 @@
                 pl.semaphore_signal(credit, inc=1, device_id={"stage": lax.rem(stage + STAGES - 1, STAGES)},
                                     device_id_type=pl.DeviceIdType.MESH)
 
-            @pl.when((stage == 0) & (i + 1 < NB))
-            def _():
-                emb_copy(i + 1).start()
+            @pl.when((stage == 0) & (i == 0))
+            def _():
+                emb_copy(1).start()
 
             @pl.when(i == 0)
             def _():

time: 416 us -> 416 us (level)
  no operation moved by 1% of the time
where the time goes in v9:
time: 416 us; the launch traced here: 415 us
  Pallas kernels  414 us (100%)
    pallas_call x1, Pallas kernels, stage_program(): pl.pallas_call(stage_kernel, name='stage_pipeline', out_shape=(jax.ShapeD...  410 us

profile of v9, /device:TPU:7, one launch (start us, length us, event | category | flops | bytes accessed | tf_op | source)
XLA Modules:
  0.0 415.5 jit_solution(12444260280744754437)
XLA Ops:
  1.3 410.2 %stage_pipeline.1 = (bf16[384,2048]{1,0:T(8,128)(2,1)}, bf16[512,1536]{1,0:T(8,128)(2,1)}, bf16[512,1536]{1,0:T(8,128)(2,1)}, bf16[2048,2048]{1,0:T(8,128)(2,1)}...) custom-call(bf16[1536,2048]{1,0:T(8,128)(2,1)} %emb.1, s32[1]{0:T(128)S(6)} %copy.15.valid, f32[1,2048]{1,0:T(1,128)} %again_hbm.1, ...), custom_call_target="tpu_custom_call" | custom-call | tf_op jit(solution)/shard_map/stage_pipeline/pallas_call | solution.py:574
  411.5 4.0 place.1
